TPU v7x, 128 devices: a whole 4x4x4 slice. The times are simulated.
128 devices in a mesh: row: 16 (over z, y), col: 8 (over x, core).
Axes of the slice: x: 4, y: 4, z: 4, core: 2. Of those that a mesh axis runs over, the one named last changes fastest.
Arguments:
- params: float32 [4, 4096, 10240], P(None, ('row', 'col'))
- grads: bfloat16 [4, 4096, 10240], P(None, ('row', 'col')), may hold values from -6 to 6
- row_state_old: float32 [4, 4096], P(None, ('row', 'col')), may hold values from 0.05 to 0.5
- col_state_old: float32 [4, 10240], P(None, ('row', 'col')), may hold values from 0.05 to 0.5
- old_map: int32 [4, 128], replicated, may hold values from 0 to 127, each once within a row
- new_map: int32 [4, 128], replicated, may hold values from 0 to 127, each once within a row
Outputs:
- new_params: float32 [4, 4096, 10240], P(None, 'row', 'col')
- step_change: float32 [4, 4096, 10240], P(None, 'row', 'col')
- row_state: float32 [4, 4096], P(None, ('row', 'col'))
- col_state: float32 [4, 10240], P(None, ('row', 'col'))
Inputs may be any that keep to these rules, and one draw needn't show every extreme that they name: Each row of old_map is a permutation of 0 to 127. Each row of new_map is a permutation of 0 to 127.
All inputs are finite; a program needn't handle non-finite values.
Results may differ from a plain program's by a relative error of at most 0.0003.
Values may be sent and summed in bfloat16 or wider, within the bound.
A program may use at most 128 MiB of HBM per device.

v0:
```python
import math

import jax
import jax.numpy as jnp
from jax import lax
from jax.sharding import Mesh
from jax.sharding import PartitionSpec as P

D = 4096
FF = 10240
STEP = 4
ROW_COL = ("row_0", "row_1", "col_0", "col_1")
ROW = ("row_0", "row_1")
COL = ("col_0", "col_1")


eps_square = 1e-30
clip_limit = 1.0
highest = lax.Precision.HIGHEST


def by_axis(x, axes):
    for axis in axes:
        x = lax.psum(x, axis)
    return x


def in_order(pieces, dim):
    dims = list(pieces.shape[1:])
    dims[dim] *= pieces.shape[0]
    return jnp.moveaxis(pieces, 0, dim).reshape(dims)


def gather_together(arrays, axis, dims):
    flat = jnp.concatenate([a.reshape(-1) for a in arrays])
    lines, at, gathered = (lax.all_gather(flat, axis), 0, [])
    for a, dim in zip(arrays, dims):
        pieces = lines[:, at : at + a.size].reshape(-1, *a.shape)
        gathered.append(in_order(pieces, dim))
        at += a.size
    return tuple(gathered)


def cut_along(x, dim, size):
    dims = x.shape
    pieces = x.reshape(*dims[:dim], size, dims[dim] // size, *dims[dim + 1 :])
    return jnp.moveaxis(pieces, dim, 0)


def cut_rows(length, count):
    unit = 8 if length >= 8 * count else 1
    return [length // unit * k // count * unit for k in range(1, count)]


def cut_exchange(x, axis, pieces, split_dim, concat_dim):
    blocks = cut_along(x, split_dim, lax.axis_size(axis))
    widest = max(range(1, max(2, blocks.ndim - 1)), key=lambda d: blocks.shape[d])
    gathered = []
    for section in jnp.split(blocks, cut_rows(blocks.shape[widest], pieces), axis=widest):
        if section.size:
            gathered.append(lax.all_to_all(section, axis, split_axis=0, concat_axis=0, tiled=True))
    return in_order(jnp.concatenate(gathered, axis=widest), concat_dim)


def sent_to_all(x, axis):
    size = lax.axis_size(axis)
    return lax.all_to_all(jnp.broadcast_to(x[None], (size, *x.shape)), axis, 0, 0, tiled=True)


def over_copies(x, axis):
    everything = sent_to_all(x, axis)
    return jnp.sum(everything, axis=0)


def packed_total(arrays, axis):
    ends = [0]
    for a in arrays:
        ends.append(ends[-1] + a.size)
    total = over_copies(jnp.concatenate([a.ravel() for a in arrays]), axis)
    return tuple((total[b:e].reshape(a.shape) for a, b, e in zip(arrays, ends, ends[1:])))


def gathered_copies(x, axis, dim):
    return in_order(sent_to_all(x, axis), dim)


def reorder(stored, order, blocks):
    matrices = stored.shape[0]
    pieces = stored.reshape(matrices, blocks, stored.shape[1] // blocks)
    onehot = (order[:, :, None] == jnp.arange(blocks, dtype=jnp.int32)[None, None, :]).astype(
        jnp.float32
    )
    return jnp.einsum("mfb,mfw->mbw", onehot, pieces, precision=highest).reshape(matrices, -1)


def select_block(whole, order, blocks, flat_index):
    matrices = whole.shape[0]
    wanted = lax.dynamic_slice_in_dim(order, flat_index, 1, 1)
    onehot = (wanted == jnp.arange(blocks, dtype=jnp.int32)[None, :]).astype(jnp.float32)
    pieces = whole.reshape(matrices, blocks, whole.shape[1] // blocks)
    return jnp.einsum("mb,mbw->mw", onehot, pieces, precision=highest)


def totals(update_part, param_part):
    update_total, param_total = (by_axis(update_part, ROW_COL), by_axis(param_part, ROW_COL))
    return (update_total, param_total)


def apply_update(weights, gradient, row_new, col_new, row_mean, step_rate):
    variance = row_new[:, :, None] * col_new[:, None, :] / row_mean[:, None, None]
    update = gradient / jnp.sqrt(variance)
    param_part = jnp.sum(weights * weights, axis=(1, 2))
    update_part = jnp.sum(update * update, axis=(1, 2))
    update_total, param_total = totals(update_part, param_part)
    count = weights.shape[0] * D * FF
    clip_factor = jnp.maximum(1.0, jnp.sqrt(jnp.sum(update_total) / count) / clip_limit)
    param_scale = jnp.sqrt(param_total / (D * FF) + 1e-06)
    change = -(step_rate * param_scale)[:, None, None] * update / clip_factor
    return (weights + change, change)


def shards(params, grads, row_state_old, col_state_old, old_map, new_map):
    decay_rate = 1.0 - float(STEP) ** (-0.8)
    step_rate = min(0.01, 1.0 / math.sqrt(STEP))
    row_count = lax.axis_size(ROW)
    col_count = lax.axis_size(COL)
    blocks = row_count * col_count
    flat_index = lax.axis_index(ROW_COL)
    stored_rows, stored_cols = gather_together((row_state_old, col_state_old), ROW_COL, (1, 1))
    row_old = reorder(stored_rows, old_map, blocks)
    col_old = reorder(stored_cols, old_map, blocks)
    old_mean = jnp.mean(row_old, axis=1)
    weights = cut_exchange(params, COL, 2, 2, 1)
    moved = lax.all_to_all(grads, COL, split_axis=2, concat_axis=1, tiled=True)
    gradient = moved.astype(jnp.float32)
    squares = gradient * gradient + eps_square
    rows_here = gradient.shape[1]
    cols_here = gradient.shape[2]
    row_total = over_copies(jnp.sum(squares, axis=2), COL)
    col_total, grand_total = packed_total(
        (jnp.sum(squares, axis=1), jnp.sum(row_total, axis=1)), ROW
    )
    row_block = lax.dynamic_slice_in_dim(row_old, lax.axis_index(ROW) * rows_here, rows_here, 1)
    col_block = lax.dynamic_slice_in_dim(col_old, lax.axis_index(COL) * cols_here, cols_here, 1)
    row_new = decay_rate * row_block + (1.0 - decay_rate) * row_total / FF
    col_new = decay_rate * col_block + (1.0 - decay_rate) * col_total / D
    row_mean = decay_rate * old_mean + (1.0 - decay_rate) * grand_total / (D * FF)
    new_params, step_change = apply_update(weights, gradient, row_new, col_new, row_mean, step_rate)
    whole_rows = gathered_copies(row_new, ROW, 1)
    whole_cols = gathered_copies(col_new, COL, 1)
    row_state = select_block(whole_rows, new_map, blocks, flat_index)
    col_state = select_block(whole_cols, new_map, blocks, flat_index)
    return (new_params, step_change, row_state, col_state)


def solution(mesh):
    torus = Mesh(mesh.devices.reshape(4, 4, 4, 2), ("row_0", "row_1", "col_0", "col_1"))
    placed = (
        P(None, ROW_COL, None),
        P(None, ROW_COL, None),
        P(None, ROW_COL),
        P(None, ROW_COL),
        P(),
        P(),
    )
    return jax.shard_map(
        shards,
        mesh=torus,
        in_specs=placed,
        out_specs=(P(None, ROW, COL), P(None, ROW, COL), P(None, ROW_COL), P(None, ROW_COL)),
        check_vma=False,
    )
```

profile of v0, /device:TPU:1, one launch (start us, length us, event | category | flops | bytes accessed | tf_op | source)
XLA Modules:
  0.0 359.8 jit_solution(2165237865159302137)
XLA Ops:
  7.2 0.0 copy-start
  7.2 13.0 %copy.56 = bf16[4,32,10240]{1,0,2:T(4,128)(2,1)} copy(bf16[4,32,10240]{2,1,0:T(8,128)(2,1)} %param.7) | data formatting | bytes 5242880 | tf_op args[1]
  20.2 12.9 %reshape.81 = bf16[8,2,81920]{2,1,0:T(2,128)(2,1)} reshape(bf16[10240,4,32]{2,1,0:T(4,128)(2,1)} %bitcast.59) | data formatting | bytes 5242880
  33.1 5.8 %all-to-all-start.2 = ((bf16[8,2,81920]{2,1,0:T(2,128)(2,1)}), bf16[8,2,81920]{2,1,0:T(2,128)(2,1)}, u32[]{:S(2)}, u32[]{:S(2)}) async-start(bf16[8,2,81920]{2,1,0:T(2,128)(2,1)} %reshape.81), calls=%async_computation.2 | async-start | bytes 5242880 | tf_op jit(solution)/shard_map/all_to_all | solution.py:134
  38.9 4.1 %copy.77 = f32[16,8,8,1280]{3,2,1,0:T(8,128)S(1)} copy(f32[16,8,8,1280]{3,1,2,0:T(8,128)} %bitcast.61) | data formatting | bytes 10485760
  43.0 0.5 bitcast_bitcast_fusion
  43.5 1.9 fusion.22
  45.4 2.3 copy.52
  47.7 23.1 %all-to-all-done.2 = bf16[8,2,81920]{2,1,0:T(2,128)(2,1)} async-done(((bf16[8,2,81920]{2,1,0:T(2,128)(2,1)}), bf16[8,2,81920]{2,1,0:T(2,128)(2,1)}, u32[]{:S(2)}, u32[]{:S(2)}) %all-to-all-start.2) | async-done | bytes 2621472 | tf_op jit(solution)/shard_map/all_to_all | solution.py:134
  70.8 4.5 %all-to-all-start = ((f32[8,4,16,1280]{3,2,1,0:T(8,128)}), f32[8,4,16,1280]{3,2,1,0:T(8,128)S(1)}, u32[]{:S(2)}, u32[]{:S(2)}) async-start(f32[8,4,16,1280]{3,2,1,0:T(8,128)} %copy.52), calls=%async_computation | async-start | bytes 5242880 | tf_op jit(solution)/shard_map/all_to_all | solution.py:61
  75.3 9.5 %reshape.82 = bf16[10240,4,32]{2,1,0:T(4,128)(2,1)} reshape(bf16[8,2,81920]{2,1,0:T(2,128)(2,1)} %all-to-all-done.2) | data formatting | bytes 5242880
  84.8 14.7 %copy.57 = f32[4,32,8,1280]{3,1,2,0:T(8,128)} copy(bf16[4,32,8,1280]{1,0,3,2:T(4,128)(2,1)} %bitcast.58) | data formatting | bytes 7864320 | tf_op jit(solution)/shard_map/convert_element_type | solution.py:135
  99.4 3.5 fusion.6
  102.9 0.1 broadcast_in_dim.10
  103.0 4.2 %all-to-all-done = f32[8,4,16,1280]{3,2,1,0:T(8,128)S(1)} async-done(((f32[8,4,16,1280]{3,2,1,0:T(8,128)}), f32[8,4,16,1280]{3,2,1,0:T(8,128)S(1)}, u32[]{:S(2)}, u32[]{:S(2)}) %all-to-all-start) | async-done | bytes 2621472 | tf_op jit(solution)/shard_map/all_to_all | solution.py:61
  107.1 0.6 broadcast_in_dim.11
  107.7 4.2 %all-to-all-start.3 = ((f32[8,4,256]{2,1,0:T(4,128)}), f32[8,4,256]{2,1,0:T(4,128)S(1)}, u32[]{:S(2)}, u32[]{:S(2)}) async-start(f32[8,4,256]{2,1,0:T(4,128)} %broadcast_in_dim.11), calls=%async_computation.3 | async-start | bytes 65536 | tf_op jit(solution)/shard_map/all_to_all | solution.py:67
  111.9 4.1 %copy.53 = f32[8,4,16,1280]{3,2,1,0:T(8,128)} copy(f32[8,4,16,1280]{3,0,2,1:T(8,128)} %get-tuple-element.19) | data formatting | bytes 5242880 | tf_op jit(solution)/shard_map/split | solution.py:59
  116.0 0.6 all-to-all-done.3
  116.7 5.0 %all-to-all-start.1 = ((f32[8,4,16,1280]{3,2,1,0:T(8,128)}), f32[8,4,16,1280]{3,2,1,0:T(8,128)}, u32[]{:S(2)}, u32[]{:S(2)}) async-start(f32[8,4,16,1280]{3,2,1,0:T(8,128)} %copy.53), calls=%async_computation.1 | async-start | bytes 5242880 | tf_op jit(solution)/shard_map/all_to_all | solution.py:61
  121.7 0.0 all-reduce.7.cloned.1.call-start
  121.7 0.1 reshape.65
  121.8 0.1 reshape.64
  121.9 0.1 maximum_dynamic-update-slice_fusion
  122.0 0.7 copy-done.1
  122.7 0.0 all-reduce.7.cloned.1.call-update
  122.7 0.2 dynamic-slice_reduce_fusion
  122.9 0.1 fusion.18
  123.0 152.0 %all-reduce.7.cloned.1.call-done = f32[57344]{0:T(1024)} async-done(((f32[57344]{0:T(1024)}), f32[57344]{0:T(1024)}) %all-reduce.7.cloned.1.call-update) | async-done | bytes 229392
  275.0 1.0 reshape.74
  276.1 0.1 copy.61
  276.3 0.5 fusion.10
  276.7 0.2 reshape.69
  277.0 0.1 copy.58
  277.1 0.4 fusion.23
  277.5 0.1 copy.59
  277.6 0.2 reshape.67
  277.8 0.1 fusion.20
  278.0 0.0 all-to-all-done.1
  278.0 0.6 broadcast_in_dim.13
  278.6 5.0 %all-to-all-start.5 = ((f32[16,4,256]{2,1,0:T(4,128)}), f32[16,4,256]{2,1,0:T(4,128)S(1)}, u32[]{:S(2)}, u32[]{:S(2)}) async-start(f32[16,4,256]{2,1,0:T(4,128)} %broadcast_in_dim.13), calls=%async_computation.5 | async-start | bytes 131072 | tf_op jit(solution)/shard_map/all_to_all | solution.py:67
  283.6 6.6 %all-to-all-done.5 = f32[16,4,256]{2,1,0:T(4,128)S(1)} async-done(((f32[16,4,256]{2,1,0:T(4,128)}), f32[16,4,256]{2,1,0:T(4,128)S(1)}, u32[]{:S(2)}, u32[]{:S(2)}) %all-to-all-start.5) | async-done | bytes 65568 | tf_op jit(solution)/shard_map/all_to_all | solution.py:67
  290.2 0.9 broadcast_in_dim.12
  291.1 3.7 %all-to-all-start.4 = ((f32[16,1,5124]{2,1,0:T(1,128)}), f32[16,1,5124]{2,1,0:T(1,128)S(1)}, u32[]{:S(2)}, u32[]{:S(2)}) async-start(f32[16,1,5124]{2,1,0:T(1,128)} %broadcast_in_dim.12), calls=%async_computation.4 | async-start | bytes 671744 | tf_op jit(solution)/shard_map/all_to_all | solution.py:67
  294.8 2.1 pad_maximum_fusion
  296.9 2.7 copy.71
  299.6 2.3 fusion.5
  301.9 0.1 mul.105
  302.0 0.1 reshape_reshape.6
  302.1 1.6 all-to-all-done.4
  303.7 0.2 reduce_sum.86
  304.0 3.5 fusion.3
  307.5 0.8 fusion.16
  308.4 7.0 %all-reduce.3 = (f32[4]{0:T(128)S(1)}, f32[4]{0:T(128)S(1)}) all-reduce(f32[4]{0:T(128)S(1)} %fusion.3, f32[4]{0:T(128)S(1)} %fusion.5), channel_id=1, replica_groups=mesh['row_0'=4,'row_1'=4,'col_0'=4,'col_1'=2] {'row_0'}, use_global_device_ids=true, to_apply=%region_12.0 | all-reduce | flops 8 | bytes 64 | tf_op jit(solution)/shard_map/psum | solution.py:24
  315.4 8.1 %all-reduce.2 = (f32[4]{0:T(128)S(1)}, f32[4]{0:T(128)S(1)}) all-reduce(f32[4]{0:T(128)S(1)} %get-tuple-element.12, f32[4]{0:T(128)S(1)} %get-tuple-element.13), channel_id=1, replica_groups=mesh['row_0'=4,'row_1'=4,'col_0'=4,'col_1'=2] {'row_1'}, use_global_device_ids=true, to_apply=%region_13.0 | all-reduce | flops 8 | bytes 64 | tf_op jit(solution)/shard_map/psum | solution.py:24
  323.5 6.7 %all-reduce.1 = (f32[4]{0:T(128)S(1)}, f32[4]{0:T(128)S(1)}) all-reduce(f32[4]{0:T(128)S(1)} %get-tuple-element.10, f32[4]{0:T(128)S(1)} %get-tuple-element.11), channel_id=1, replica_groups=mesh['row_0'=4,'row_1'=4,'col_0'=4,'col_1'=2] {'col_0'}, use_global_device_ids=true, to_apply=%region_14.0 | all-reduce | flops 8 | bytes 64 | tf_op jit(solution)/shard_map/psum | solution.py:24
  330.2 8.8 %all-reduce.4 = (f32[4]{0:T(128)S(1)}, f32[4]{0:T(128)S(1)}) all-reduce(f32[4]{0:T(128)S(1)} %get-tuple-element.8, f32[4]{0:T(128)S(1)} %get-tuple-element.9), channel_id=1, replica_groups=mesh['row_0'=4,'row_1'=4,'col_0'=4,'col_1'=2] {'col_1'}, use_global_device_ids=true, to_apply=%region_15.0 | all-reduce | flops 8 | bytes 64 | tf_op jit(solution)/shard_map/psum | solution.py:24
  339.0 0.6 reduce_sum.89
  340.4 0.7 broadcast_in_dim.14
  341.0 3.6 %all-to-all-start.6 = ((f32[8,4,1280]{2,1,0:T(4,128)}), f32[8,4,1280]{2,1,0:T(4,128)S(1)}, u32[]{:S(2)}, u32[]{:S(2)}) async-start(f32[8,4,1280]{2,1,0:T(4,128)} %broadcast_in_dim.14), calls=%async_computation.6 | async-start | bytes 327680 | tf_op jit(solution)/shard_map/all_to_all | solution.py:67
  344.7 7.3 %bitcast_add_fusion = (f32[4,256,1280]{2,1,0:T(8,128)}, f32[4,256,1280]{2,1,0:T(8,128)}) fusion(f32[8,4,32,1280]{3,2,0,1:T(8,128)} %copy.71, f32[]{:T(128)S(6)} %max.3, f32[4]{0:T(128)S(1)} %fusion.19, f32[4,1280]{1,0:T(4,128)S(1)} %multiply_add_fusion, f32[4,256]{1,0:T(4,128)S(1)} %multiply_add_fusion.1, f32[4,32,8,1280]{3,1,2,0:T(8,128)} %copy.57, ...), kind=kLoop, calls=%fused_computation.5 | loop fusion | flops 7864320 | bytes 20996132 | tf_op jit(solution)/shard_map/add | solution.py:119
  351.9 0.0 all-to-all-done.6
  352.0 0.2 reshape_reshape.7
  352.1 0.8 fusion.14
  (21 shorter events, 0.2 us)
Async XLA Ops:
  7.2 115.6 %copy-start = (s32[4,128]{1,0:T(4,128)S(1)}, s32[4,128]{1,0:T(4,128)}, u32[]{:S(2)}) copy-start(s32[4,128]{1,0:T(4,128)} %param.11) | copy-start | bytes 6148
  33.1 37.7 %all-to-all-start.2 = ((bf16[8,2,81920]{2,1,0:T(2,128)(2,1)}), bf16[8,2,81920]{2,1,0:T(2,128)(2,1)}, u32[]{:S(2)}, u32[]{:S(2)}) async-start(bf16[8,2,81920]{2,1,0:T(2,128)(2,1)} %reshape.81), calls=%async_computation.2 | async-start | bytes 5242880 | tf_op jit(solution)/shard_map/all_to_all | solution.py:134
  70.8 36.4 %all-to-all-start = ((f32[8,4,16,1280]{3,2,1,0:T(8,128)}), f32[8,4,16,1280]{3,2,1,0:T(8,128)S(1)}, u32[]{:S(2)}, u32[]{:S(2)}) async-start(f32[8,4,16,1280]{3,2,1,0:T(8,128)} %copy.52), calls=%async_computation | async-start | bytes 5242880 | tf_op jit(solution)/shard_map/all_to_all | solution.py:61
  107.7 8.9 %all-to-all-start.3 = ((f32[8,4,256]{2,1,0:T(4,128)}), f32[8,4,256]{2,1,0:T(4,128)S(1)}, u32[]{:S(2)}, u32[]{:S(2)}) async-start(f32[8,4,256]{2,1,0:T(4,128)} %broadcast_in_dim.11), calls=%async_computation.3 | async-start | bytes 65536 | tf_op jit(solution)/shard_map/all_to_all | solution.py:67
  111.9 9.8 %copy-start.4 = (f32[4,80]{1,0:T(4,128)S(1)}, f32[4,80]{1,0:T(4,128)}, u32[]{:S(2)}) copy-start(f32[4,80]{1,0:T(4,128)} %param.9) | copy-start | bytes 3844
  111.9 9.8 %copy-start.3 = (f32[4,32]{1,0:T(4,128)S(1)}, f32[4,32]{1,0:T(4,128)}, u32[]{:S(2)}) copy-start(f32[4,32]{1,0:T(4,128)} %param.8) | copy-start | bytes 1540
  111.9 164.3 %copy-start.2 = (s32[4,128]{1,0:T(4,128)S(1)}, s32[4,128]{1,0:T(4,128)}, u32[]{:S(2)}) copy-start(s32[4,128]{1,0:T(4,128)} %param.10) | copy-start | bytes 6148
  116.7 161.3 %all-to-all-start.1 = ((f32[8,4,16,1280]{3,2,1,0:T(8,128)}), f32[8,4,16,1280]{3,2,1,0:T(8,128)}, u32[]{:S(2)}, u32[]{:S(2)}) async-start(f32[8,4,16,1280]{3,2,1,0:T(8,128)} %copy.53), calls=%async_computation.1 | async-start | bytes 5242880 | tf_op jit(solution)/shard_map/all_to_all | solution.py:61
  121.7 153.4 %all-reduce.7.cloned.1.call-start = ((), (), s32[]{:S(2)}) async-start(), calls=%async_computation.7 | async-start | bytes 458752
  122.0 0.7 copy-start.1
  278.6 11.6 %all-to-all-start.5 = ((f32[16,4,256]{2,1,0:T(4,128)}), f32[16,4,256]{2,1,0:T(4,128)S(1)}, u32[]{:S(2)}, u32[]{:S(2)}) async-start(f32[16,4,256]{2,1,0:T(4,128)} %broadcast_in_dim.13), calls=%async_computation.5 | async-start | bytes 131072 | tf_op jit(solution)/shard_map/all_to_all | solution.py:67
  291.1 12.6 %all-to-all-start.4 = ((f32[16,1,5124]{2,1,0:T(1,128)}), f32[16,1,5124]{2,1,0:T(1,128)S(1)}, u32[]{:S(2)}, u32[]{:S(2)}) async-start(f32[16,1,5124]{2,1,0:T(1,128)} %broadcast_in_dim.12), calls=%async_computation.4 | async-start | bytes 671744 | tf_op jit(solution)/shard_map/all_to_all | solution.py:67
  341.0 10.9 %all-to-all-start.6 = ((f32[8,4,1280]{2,1,0:T(4,128)}), f32[8,4,1280]{2,1,0:T(4,128)S(1)}, u32[]{:S(2)}, u32[]{:S(2)}) async-start(f32[8,4,1280]{2,1,0:T(4,128)} %broadcast_in_dim.14), calls=%async_computation.6 | async-start | bytes 327680 | tf_op jit(solution)/shard_map/all_to_all | solution.py:67
Sparse Core Ops, SparseCore 0:
  127.8 147.1 all-reduce.6
where the time goes:
time: 362 us; the launch traced here: 360 us
  waiting for transfers between devices  188 us (52%)
  local copies, waits for them, and re-layouts  71.8 us (20%)
  starting transfers between devices  31.8 us (9%)
  blocking collectives  30.7 us (8%)
  other arithmetic  19.8 us (5%)
  between operations  15 us (4%)
    unnamed x2, waiting for transfers between devices  152 us
    unnamed x15, local copies, waits for them, and re-layouts  40.2 us
    psum x4, blocking collectives, by_axis(): x = lax.psum(x, axis)  30.7 us
    all_to_all x1, waiting for transfers between devices, shards(): moved = lax.all_to_all(grads, COL, split_axis=2, concat_axis=1, tiled=True)  23.1 us
    all_to_all x4, starting transfers between devices, sent_to_all(): lax.all_to_all(jnp.broadcast_to(x[None], (size, *x.shape)), axis, 0, 0, t...  16.5 us
    convert_element_type x1, local copies, waits for them, and re-layouts, shards(): gradient = moved.astype(jnp.float32)  14.7 us
    all_to_all x2, starting transfers between devices, cut_exchange(): lax.all_to_all(section, axis, split_axis=0, concat_axis=0, tiled=True)  9.51 us
    all_to_all x4, waiting for transfers between devices, sent_to_all(): lax.all_to_all(jnp.broadcast_to(x[None], (size, *x.shape)), axis, 0, 0, t...  8.83 us
  transfers between devices with their start and end apart: 8, of which 6 were waited for; matrix products, arithmetic and copies ran while one was open for 16% of the time, Pallas kernels for 0%

commit v1 on v0

v1 whole, which is shorter than its diff:
```python
import functools
import math

import jax
import jax.numpy as jnp
from jax import lax
from jax.experimental import pallas as pl
from jax.experimental.pallas import tpu as pltpu
from jax.sharding import Mesh
from jax.sharding import PartitionSpec as P

D = 4096
FF = 10240
STEP = 4
M = 4
ROWS = 32
COLS = 1280
AXES = ("z", "y", "x", "c")
MESH = pl.DeviceIdType.MESH
HIGHEST = lax.Precision.HIGHEST
DECAY = 1.0 - float(STEP) ** (-0.8)
RATE = min(0.01, 1.0 / math.sqrt(STEP))
EPS = 1e-30
F32 = jnp.float32
FIRST = 1

COL_PEERS = [(1, 0), (3, 0), (2, 0), (1, 1), (3, 1), (2, 1), (0, 1)]
LINE_PEERS = [1, 2, 3]


def iota(shape, dim):
    return lax.broadcasted_iota(jnp.int32, shape, dim)


def exchange_kernel(
    params, grads, row_old, col_old, old_map,
    p_out, g_out, r_out, c_out, rows_out, cols_out,
    gv, pv, stored, row_tiles, red_y, red_z, sc_x, sc_y, sc_z, sel, rnew,
    load_sem, own_sem,
    s_tile, r_tile, s_line, r_line, s_grad, r_grad, s_par, r_par,
    s_row, r_row, s_red, r_red, s_sc, r_sc, s_col, r_col,
):
    z, y, x, c = (lax.axis_index(a) for a in AXES)
    k = x * 2 + c
    f = (z * 4 + y) * 8 + k

    def col_peer(i):
        dx, dc = COL_PEERS[i]
        return lax.rem(x + dx, 4), lax.rem(c + dc, 2)

    def to_cols(i, src, dst, ss, rs):
        tx, tc = col_peer(i)
        return pltpu.make_async_remote_copy(
            src_ref=src, dst_ref=dst, send_sem=ss, recv_sem=rs,
            device_id={"x": tx, "c": tc}, device_id_type=MESH,
        )

    def to_line(axis, d, src, dst, ss, rs):
        at = lax.rem((y if axis == "y" else z) + d, 4)
        return pltpu.make_async_remote_copy(
            src_ref=src, dst_ref=dst, send_sem=ss, recv_sem=rs,
            device_id={axis: at}, device_id_type=MESH,
        )

    def begin(copies):
        for cp in copies:
            cp.start()
        return copies

    def arrive(copies):
        for cp in copies:
            cp.wait_recv()

    loads = []
    for m in range(M):
        loads.append(pltpu.make_async_copy(grads.at[m], gv.at[m], load_sem.at[m]))
    for m in range(M):
        loads.append(pltpu.make_async_copy(params.at[m], pv.at[m], load_sem.at[M + m]))
    begin(loads)

    barrier = pltpu.get_barrier_semaphore()
    for i in range(7):
        tx, tc = col_peer(i)
        pl.semaphore_signal(barrier, inc=1, device_id={"x": tx, "c": tc}, device_id_type=MESH)
    for d in LINE_PEERS:
        pl.semaphore_signal(barrier, inc=1, device_id={"y": lax.rem(y + d, 4)}, device_id_type=MESH)
        pl.semaphore_signal(barrier, inc=1, device_id={"z": lax.rem(z + d, 4)}, device_id_type=MESH)

    mine = stored.at[pl.ds(pl.multiple_of(f * 8, 8), 8)]
    mine[...] = jnp.zeros((8, 128), F32)
    mine[0:4, 0:80] = col_old[...]
    mine[4:8, 0:32] = row_old[...]

    pl.semaphore_wait(barrier, 13)

    tiles = begin([to_cols(i, mine, mine, s_tile.at[i], r_tile.at[i]) for i in range(7)])
    sent = list(tiles)

    def columns(i):
        tx, tc = col_peer(i)
        return pl.ds(pl.multiple_of((tx * 2 + tc) * COLS, 128), COLS)

    grad_copies = begin(
        [to_cols(i, grads.at[:, :, columns(i)], g_out.at[k], s_grad.at[i], r_grad.at[i]) for i in range(7)]
    )
    sent += grad_copies

    def send_params(m):
        copies = begin(
            [
                to_cols(i, params.at[m, :, columns(i)], p_out.at[k, m], s_par.at[m, i], r_par.at[m, i])
                for i in range(7)
            ]
        )
        sent.extend(copies)
        return copies

    par_copies = []
    for m in range(FIRST):
        par_copies += send_params(m)

    own_columns = pl.ds(pl.multiple_of(k * COLS, 128), COLS)
    lane32 = iota((ROWS, 128), 1)
    row_sums = jnp.zeros((ROWS, 128), F32)
    own = []
    for m in range(M):
        loads[m].wait()

        def add_squares(t, acc, m=m):
            g = gv[m, :, pl.ds(pl.multiple_of(t * COLS, 128), COLS)].astype(F32)
            sq = g * g + EPS
            for u in range(COLS // 128):
                acc = acc + sq[:, u * 128 : (u + 1) * 128]
            return acc

        part = lax.fori_loop(0, 8, add_squares, jnp.zeros((ROWS, 128), F32))
        total = jnp.sum(part, axis=1, keepdims=True)
        row_sums = row_sums + jnp.where(lane32 == m, total, 0.0)
        own.append(pltpu.make_async_copy(gv.at[m, :, own_columns], g_out.at[k, m], own_sem.at[m]))
        own[-1].start()

    arrive(tiles)
    line_at = stored.at[pl.ds(pl.multiple_of((z * 4 + y) * 64, 64), 64)]
    lines = begin([to_line("y", d, line_at, line_at, s_line.at[d - 1], r_line.at[d - 1]) for d in LINE_PEERS])
    sent += lines

    lane8 = iota((8, 128), 1)
    squares = jnp.zeros((8, 128), F32)
    for m in range(M):
        loads[M + m].wait()

        def add_weights(t, acc, m=m):
            w = pv[m, :, pl.ds(pl.multiple_of(t * COLS, 128), COLS)]
            sq = w * w
            for u in range(COLS // 128):
                for v in range(ROWS // 8):
                    acc = acc + sq[v * 8 : (v + 1) * 8, u * 128 : (u + 1) * 128]
            return acc

        part = lax.fori_loop(0, 8, add_weights, jnp.zeros((8, 128), F32))
        total = jnp.sum(jnp.sum(part, axis=1, keepdims=True), axis=0, keepdims=True)
        squares = squares + jnp.where(lane8 == m, total, 0.0)
        own.append(pltpu.make_async_copy(pv.at[m, :, own_columns], p_out.at[k, m], own_sem.at[M + m]))
        own[-1].start()

    arrive(lines)
    slab_at = stored.at[pl.ds(pl.multiple_of(z * 256, 256), 256)]
    slabs = begin([to_line("z", d, slab_at, slab_at, s_line.at[d + 2], r_line.at[d + 2]) for d in LINE_PEERS])
    sent += slabs
    arrive(slabs)

    at_row = iota((128, 128), 0)
    picked = jnp.zeros((128, 128), F32)
    for m in range(M):
        onehot = jnp.where((at_row == m) & (old_map[m : m + 1, :] == f), 1.0, 0.0)
        picked = picked + jnp.dot(
            onehot, stored[pl.ds(4 + m, 128, stride=8), :], precision=HIGHEST, preferred_element_type=F32
        )
    row_block = jnp.transpose(picked)[0:ROWS, :]
    row_new = DECAY * row_block + (1.0 - DECAY) * row_sums / FF
    row_tiles[k, 0:ROWS, :] = jnp.where(lane32 < M, row_new, 1.0)
    row_tiles[k, ROWS : ROWS + 8, :] = jnp.where(iota((8, 128), 0) == 0, squares, 0.0)
    row_copies = begin(
        [to_cols(i, row_tiles.at[k], row_tiles.at[k], s_row.at[i], r_row.at[i]) for i in range(7)]
    )
    sent += row_copies

    lane = iota((1, COLS), 1)
    block_of = ((lane.astype(F32) + 0.5) * (1.0 / 80.0)).astype(jnp.int32)
    place_of = lane - 80 * block_of
    at64 = iota((64, 128), 0)
    blocks = jnp.zeros((64, 128), F32)
    for m in range(M):
        wanted = (at64 - 16 * m) + k * 16
        inside = (at64 >= 16 * m) & (at64 < 16 * m + 16)
        onehot = jnp.where(inside & (old_map[m : m + 1, :] == wanted), 1.0, 0.0)
        blocks = blocks + jnp.dot(
            onehot, stored[pl.ds(m, 128, stride=8), :], precision=HIGHEST, preferred_element_type=F32
        )
    sel[0:64, 0:128] = blocks
    spread = jnp.where(iota((128, COLS), 0) == place_of, 1.0, 0.0)
    wide = jnp.dot(sel[0:64, 0:128], spread, precision=HIGHEST, preferred_element_type=F32)
    sel[...] = wide
    at16 = iota((16, COLS), 0)
    old_cols = [
        jnp.sum(jnp.where(at16 == block_of, sel[m * 16 : (m + 1) * 16, :], 0.0), axis=0, keepdims=True)
        for m in range(M)
    ]
    for m in range(M):
        c_out[m : m + 1, :] = old_cols[m]

    arrive(grad_copies)
    for m in range(M):
        own[m].wait()

    red_y[y, 4:8, :] = jnp.zeros((4, COLS), F32)
    for m in range(M):

        def add_columns(t, acc, m=m):
            g = g_out[t, m].astype(F32)
            sq = g * g + EPS
            for v in range(ROWS // 8):
                acc = acc + sq[v * 8 : (v + 1) * 8, :]
            return acc

        part = lax.fori_loop(0, 8, add_columns, jnp.zeros((8, COLS), F32))
        red_y[y, m : m + 1, :] = jnp.sum(part, axis=0, keepdims=True)

    arrive(row_copies)
    row_sum = jnp.zeros((1, 128), F32)
    weight_sum = jnp.zeros((1, 128), F32)
    for t in range(8):
        part = row_tiles[t, 0:ROWS, :]
        rnew[t * ROWS : (t + 1) * ROWS, :] = part
        row_sum = row_sum + jnp.sum(part, axis=0, keepdims=True)
        weight_sum = weight_sum + row_tiles[t, ROWS : ROWS + 1, :]
    red_y[y, 4:5, 0:128] = row_sum
    red_y[y, 5:6, 0:128] = weight_sum
    across = jnp.transpose(rnew[0:128, :]), jnp.transpose(rnew[128:256, :])
    own_row = z * 4 + y
    rows_out[own_row, :, 0:128] = across[0][0:8, :]
    rows_out[own_row, :, 128:256] = across[1][0:8, :]

    stage = begin(
        [to_line("y", d, red_y.at[y], red_y.at[y], s_red.at[d - 1], r_red.at[d - 1]) for d in LINE_PEERS]
    )
    own_rows = rows_out.at[pl.ds(own_row, 1)]
    rows_y = begin(
        [to_line("y", d, own_rows, own_rows, s_red.at[d + 5], r_red.at[d + 5]) for d in LINE_PEERS]
    )
    arrive(stage)
    sent += stage + rows_y
    red_z[z] = red_y[0] + red_y[1] + red_y[2] + red_y[3]
    stage = begin(
        [to_line("z", d, red_z.at[z], red_z.at[z], s_red.at[d + 2], r_red.at[d + 2]) for d in LINE_PEERS]
    )
    arrive(rows_y)
    slab_rows = rows_out.at[pl.ds(pl.multiple_of(z * 4, 4), 4)]
    rows_z = begin(
        [to_line("z", d, slab_rows, slab_rows, s_red.at[d + 8], r_red.at[d + 8]) for d in LINE_PEERS]
    )
    arrive(stage)
    sent += stage + rows_z
    total = red_z[0] + red_z[1] + red_z[2] + red_z[3]

    row_mean = total[4:5, 0:128] / D
    param_scale = jnp.sqrt(total[5:6, 0:128] / (D * FF) + 1e-6)
    col_new = DECAY * c_out[0:M, :] + (1.0 - DECAY) * total[0:M, :] / D
    cols_out[k] = col_new
    sel[0:M, :] = 1.0 / col_new

    update_sum = jnp.zeros((8, 128), F32)
    for m in range(M):
        inv_col = sel[m : m + 1, :]

        def add_updates(t, acc, m=m, inv_col=inv_col):
            g = g_out[t, m].astype(F32)
            sq = g * g * inv_col
            part = sq[:, 0:128]
            for u in range(1, COLS // 128):
                part = part + sq[:, u * 128 : (u + 1) * 128]
            rows = rnew[pl.ds(pl.multiple_of(t * ROWS, ROWS), ROWS), :][:, m : m + 1]
            part = part / rows
            for v in range(ROWS // 8):
                acc = acc + part[v * 8 : (v + 1) * 8, :]
            return acc

        part = lax.fori_loop(0, 8, add_updates, jnp.zeros((8, 128), F32))
        update_sum = update_sum + part * row_mean[0:1, m : m + 1]
    sc_x[k] = update_sum
    sums = begin([to_cols(i, sc_x.at[k], sc_x.at[k], s_sc.at[i], r_sc.at[i]) for i in range(7)])
    col_copies = begin(
        [to_cols(i, cols_out.at[k], cols_out.at[k], s_col.at[i], r_col.at[i]) for i in range(7)]
    )
    sent += sums + col_copies

    for m in range(FIRST, M):
        par_copies += send_params(m)

    arrive(sums)
    update_sum = sc_x[0]
    for t in range(1, 8):
        update_sum = update_sum + sc_x[t]
    sc_y[y] = update_sum
    stage = begin(
        [to_line("y", d, sc_y.at[y], sc_y.at[y], s_sc.at[d + 6], r_sc.at[d + 6]) for d in LINE_PEERS]
    )
    arrive(stage)
    sent += stage
    sc_z[z] = sc_y[0] + sc_y[1] + sc_y[2] + sc_y[3]
    stage = begin(
        [to_line("z", d, sc_z.at[z], sc_z.at[z], s_sc.at[d + 9], r_sc.at[d + 9]) for d in LINE_PEERS]
    )
    arrive(stage)
    sent += stage
    update_sum = sc_z[0] + sc_z[1] + sc_z[2] + sc_z[3]
    update_total = jnp.sum(jnp.sum(update_sum, axis=1, keepdims=True), axis=0, keepdims=True)
    clip = jnp.maximum(1.0, jnp.sqrt(update_total / (M * D * FF)))
    factor = -(RATE * param_scale) / clip * jnp.sqrt(row_mean)
    r_out[...] = factor / jnp.sqrt(rnew[...])
    c_out[0:M, :] = jnp.sqrt(sel[0:M, :])

    arrive(rows_z)
    arrive(col_copies)
    for m in range(M):
        own[M + m].wait()
    arrive(par_copies)
    for cp in sent:
        cp.wait_send()


def apply_kernel(quarter, q_ref, g_ref, r_ref, c_ref, rows_ref, cols_ref, map_ref, new_ref, change_ref, row_ref, col_ref):
    i = pl.program_id(0)
    m = i // quarter
    at = lax.rem(i, quarter)
    slots = 8 // quarter

    @pl.when(i == 0)
    def _():
        f = lax.axis_index(AXES)
        for n in range(M):
            b = map_ref[n, f]
            row = rows_ref[b // 8, n : n + 1, :]
            start = lax.rem(b, 8) * 32
            take = jnp.where(iota((256, 128), 0) == start + iota((256, 128), 1), 1.0, 0.0)
            got = jnp.dot(jnp.broadcast_to(row, (8, 256)), take, precision=HIGHEST, preferred_element_type=F32)
            row_ref[n : n + 1, :] = got[0:1, 0:32]
            col = cols_ref[b // 16, n : n + 1, :]
            start = lax.rem(b, 16) * 80
            take = jnp.where(iota((COLS, 128), 0) == start + iota((COLS, 128), 1), 1.0, 0.0)
            got = jnp.dot(jnp.broadcast_to(col, (8, COLS)), take, precision=HIGHEST, preferred_element_type=F32)
            col_ref[n : n + 1, :] = got[0:1, 0:80]

    lane = iota((ROWS, 128), 1)
    by_col = c_ref[pl.ds(m, 1), :]
    for s in range(slots):
        t = at * slots + s
        by_row = r_ref[pl.ds(pl.multiple_of(t * ROWS, ROWS), ROWS), :]
        by_row = jnp.sum(jnp.where(lane == m, by_row, 0.0), axis=1, keepdims=True)
        g = g_ref[t, m].astype(F32)
        change = (g * by_row) * by_col
        change_ref[0, s * ROWS : (s + 1) * ROWS, :] = change
        new_ref[0, s * ROWS : (s + 1) * ROWS, :] = q_ref[t, m] + change


def shards(params, grads, row_state_old, col_state_old, old_map, new_map):
    vmem = pl.BlockSpec(memory_space=pltpu.VMEM)
    hbm = pl.BlockSpec(memory_space=pl.ANY)
    dma = pltpu.SemaphoreType.DMA
    moved = pl.pallas_call(
        exchange_kernel,
        out_shape=[
            jax.ShapeDtypeStruct((8, M, ROWS, COLS), F32),
            jax.ShapeDtypeStruct((8, M, ROWS, COLS), jnp.bfloat16),
            jax.ShapeDtypeStruct((256, 128), F32),
            jax.ShapeDtypeStruct((8, COLS), F32),
            jax.ShapeDtypeStruct((16, 8, 256), F32),
            jax.ShapeDtypeStruct((8, M, COLS), F32),
        ],
        in_specs=[hbm, hbm, vmem, vmem, vmem],
        out_specs=[vmem] * 6,
        scratch_shapes=[
            pltpu.VMEM((M, ROWS, FF), jnp.bfloat16),
            pltpu.VMEM((M, ROWS, FF), F32),
            pltpu.VMEM((1024, 128), F32),
            pltpu.VMEM((8, ROWS + 8, 128), F32),
            pltpu.VMEM((4, 8, COLS), F32),
            pltpu.VMEM((4, 8, COLS), F32),
            pltpu.VMEM((8, 8, 128), F32),
            pltpu.VMEM((4, 8, 128), F32),
            pltpu.VMEM((4, 8, 128), F32),
            pltpu.VMEM((64, COLS), F32),
            pltpu.VMEM((256, 128), F32),
            dma((2 * M,)),
            dma((2 * M,)),
            dma((7,)), dma((7,)),
            dma((6,)), dma((6,)),
            dma((7,)), dma((7,)),
            dma((M, 7)), dma((M, 7)),
            dma((7,)), dma((7,)),
            dma((12,)), dma((12,)),
            dma((13,)), dma((13,)),
            dma((7,)), dma((7,)),
        ],
        compiler_params=pltpu.CompilerParams(
            collective_id=0, has_side_effects=True, vmem_limit_bytes=56 << 20
        ),
        name="exchange",
    )(params, grads, row_state_old, col_state_old, old_map)
    quarter = 4
    rows = 256 // quarter
    whole = pl.BlockSpec((1, rows, COLS), lambda i: (i // quarter, lax.rem(i, quarter), 0))
    return pl.pallas_call(
        functools.partial(apply_kernel, quarter),
        grid=(M * quarter,),
        out_shape=[
            jax.ShapeDtypeStruct((M, 256, COLS), F32),
            jax.ShapeDtypeStruct((M, 256, COLS), F32),
            jax.ShapeDtypeStruct((M, 32), F32),
            jax.ShapeDtypeStruct((M, 80), F32),
        ],
        in_specs=[vmem] * 6 + [pl.BlockSpec(memory_space=pltpu.SMEM)],
        out_specs=[
            whole,
            whole,
            pl.BlockSpec((M, 32), lambda i: (0, 0)),
            pl.BlockSpec((M, 80), lambda i: (0, 0)),
        ],
        compiler_params=pltpu.CompilerParams(vmem_limit_bytes=56 << 20),
        name="apply",
    )(*moved, new_map)


def solution(mesh):
    torus = Mesh(mesh.devices.reshape(4, 4, 4, 2), AXES)
    over = ("z", "y", "x", "c")
    return jax.shard_map(
        shards,
        mesh=torus,
        in_specs=(P(None, over, None), P(None, over, None), P(None, over), P(None, over), P(), P()),
        out_specs=(
            P(None, ("z", "y"), ("x", "c")),
            P(None, ("z", "y"), ("x", "c")),
            P(None, over),
            P(None, over),
        ),
        check_vma=False,
    )
```

time: 362 us -> 131 us (0.36)
  waiting for transfers between devices: 188 us -> 0 us
  Pallas kernels: 0 us -> 130 us
  local copies, waits for them, and re-layouts: 71.8 us -> 0 us
  starting transfers between devices: 31.8 us -> 0 us
  blocking collectives: 30.7 us -> 0 us
  other arithmetic: 19.8 us -> 0 us
  between operations: 15 us -> 0.64 us
    unnamed x2 -> x0, waiting for transfers between devices: 152 us -> none
    pallas_call x0 -> x2, Pallas kernels: none -> 130 us  [the longest x1 117 us: shards(): pl.pallas_call(exchange_kernel, out_shape=[jax.ShapeDtypeStruct((8, M, RO...]
    unnamed x15 -> x0, local copies, waits for them, and re-layouts: 40.2 us -> none
    all_to_all x7 -> x0, waiting for transfers between devices: 36.1 us -> none  [the longest x1 23.1 us: shards(): moved = lax.all_to_all(grads, COL, split_axis=2, concat_axis=1, tiled=True)]
    all_to_all x7 -> x0, starting transfers between devices: 31.8 us -> none  [the longest x4 16.5 us: sent_to_all(): lax.all_to_all(jnp.broadcast_to(x[None], (size, *x.shape)), axis, 0, 0, t...]
    psum x4 -> x0, blocking collectives: 30.7 us -> none  [by_axis(): x = lax.psum(x, axis)]
    convert_element_type x1 -> x0, local copies, waits for them, and re-layouts: 14.7 us -> none  [shards(): gradient = moved.astype(jnp.float32)]
    reduce_sum x6 -> x0, other arithmetic: 10.2 us -> none  [the longest x1 3.53 us: apply_update(): update_part = jnp.sum(update * update, axis=(1, 2))]
  transfers between devices with their start and end apart: 8 -> 0, of which waited for: 6 -> 0; matrix products, arithmetic and copies ran while one was open for 16% -> 0% of each run, Pallas kernels for 0% -> 0%
where the time goes in v1:
time: 131 us
  Pallas kernels  130 us (99%)
    pallas_call x1, Pallas kernels, shards(): pl.pallas_call(exchange_kernel, out_shape=[jax.ShapeDtypeStruct((8, M, RO...  117 us
    pallas_call x1, Pallas kernels, shards(): pl.pallas_call(functools.partial(apply_kernel, quarter), grid=(M * quarte...  12.9 us

profile of v1, /device:TPU:1, one launch (start us, length us, event | category | flops | bytes accessed | tf_op | source)
XLA Modules:
  0.0 130.8 jit_solution(534038219287304623)
XLA Ops:
  0.6 117.2 %exchange.1 = (f32[8,4,32,1280]{3,2,1,0:T(8,128)}, bf16[8,4,32,1280]{3,2,1,0:T(8,128)(2,1)}, f32[256,128]{1,0:T(8,128)}, f32[8,1280]{1,0:T(8,128)}, f32[16,8,256]{2,1,0:T(8,128)}, /*index=5*/f32[8,4,1280]{2,1,0:T(4,128)}) custom-call(f32[4,32,10240]{2,1,0:T(8,128)} %params.1, bf16[4,32,10240]{2,1,0:T(8,128)(2,1)} %grads.1, f32[4,32]{1,0:T(4,128)} %row_old.1, ...), custom_call_target="tpu_custom_call" | custom-call | tf_op jit(solution)/shard_map/exchange/pallas_call | solution.py:370
  117.9 12.9 %apply.1 = (f32[4,256,1280]{2,1,0:T(8,128)}, f32[4,256,1280]{2,1,0:T(8,128)}, f32[4,32]{1,0:T(4,128)}, f32[4,80]{1,0:T(4,128)}) custom-call(f32[8,4,32,1280]{3,2,1,0:T(8,128)} %get-tuple-element.10.q_ref, bf16[8,4,32,1280]{3,2,1,0:T(8,128)(2,1)} %get-tuple-element.11.g_ref, f32[256,128]{1,0:T(8,128)} %get-tuple-element.12.r_ref, ...), custom_call_target="tpu_custom_call" | custom-call | tf_op jit(solution)/shard_map/apply/pallas_call | solution.py:413

commit v2 on v1

v2 whole, which is shorter than its diff:
```python
import functools
import math

import jax
import jax.numpy as jnp
from jax import lax
from jax.experimental import pallas as pl
from jax.experimental.pallas import tpu as pltpu
from jax.sharding import Mesh
from jax.sharding import PartitionSpec as P

D = 4096
FF = 10240
STEP = 4
M = 4
ROWS = 32
COLS = 1280
AXES = ("z", "y", "x", "c")
MESH = pl.DeviceIdType.MESH
HIGHEST = lax.Precision.HIGHEST
DECAY = 1.0 - float(STEP) ** (-0.8)
RATE = min(0.01, 1.0 / math.sqrt(STEP))
EPS = 1e-30
F32 = jnp.float32
TOP = 32767.0
CODED = False
FIRST = 2

COL_PEERS = [(1, 0), (3, 0), (2, 0), (1, 1), (3, 1), (2, 1), (0, 1)]
LINE_PEERS = [1, 2, 3]


def iota(shape, dim):
    return lax.broadcasted_iota(jnp.int32, shape, dim)


def exchange_kernel(
    params, grads, row_hbm, col_hbm, map_hbm,
    p_out, s_out, g_out, r_out, c_out, rows_out, cols_out,
    gv, pv, qv, sv, row_old, col_old, old_map, stored, row_tiles, red_y, red_z, sc_y, sc_z, sel, rnew,
    load_sem, small_sem, own_sem,
    s_tile, r_tile, s_line, r_line, s_grad, r_grad, s_par, r_par,
    s_row, r_row, s_red, r_red, s_sc, r_sc,
):
    z, y, x, c = (lax.axis_index(a) for a in AXES)
    k = x * 2 + c
    f = (z * 4 + y) * 8 + k

    def col_peer(i):
        dx, dc = COL_PEERS[i]
        return lax.rem(x + dx, 4), lax.rem(c + dc, 2)

    def to_cols(i, src, dst, ss, rs):
        tx, tc = col_peer(i)
        return pltpu.make_async_remote_copy(
            src_ref=src, dst_ref=dst, send_sem=ss, recv_sem=rs,
            device_id={"x": tx, "c": tc}, device_id_type=MESH,
        )

    def to_line(axis, d, src, dst, ss, rs):
        at = lax.rem((y if axis == "y" else z) + d, 4)
        return pltpu.make_async_remote_copy(
            src_ref=src, dst_ref=dst, send_sem=ss, recv_sem=rs,
            device_id={axis: at}, device_id_type=MESH,
        )

    def begin(copies):
        for cp in copies:
            cp.start()
        return copies

    def arrive(copies):
        for cp in copies:
            cp.wait_recv()

    small = [
        pltpu.make_async_copy(row_hbm, row_old, small_sem.at[0]),
        pltpu.make_async_copy(col_hbm, col_old, small_sem.at[1]),
        pltpu.make_async_copy(map_hbm, old_map, small_sem.at[2]),
    ]
    begin(small)
    loads = []
    for m in range(M):
        loads.append(pltpu.make_async_copy(grads.at[m], gv.at[m], load_sem.at[m]))
    for m in range(M):
        loads.append(pltpu.make_async_copy(params.at[m], pv.at[m], load_sem.at[M + m]))
    begin(loads)

    barrier = pltpu.get_barrier_semaphore()
    for i in range(7):
        tx, tc = col_peer(i)
        pl.semaphore_signal(barrier, inc=1, device_id={"x": tx, "c": tc}, device_id_type=MESH)
    for d in LINE_PEERS:
        pl.semaphore_signal(barrier, inc=1, device_id={"y": lax.rem(y + d, 4)}, device_id_type=MESH)
        pl.semaphore_signal(barrier, inc=1, device_id={"z": lax.rem(z + d, 4)}, device_id_type=MESH)

    mine = stored.at[pl.ds(pl.multiple_of(f * 8, 8), 8)]
    mine[...] = jnp.zeros((8, 128), F32)
    for cp in small:
        cp.wait()
    mine[0:4, 0:80] = col_old[...]
    mine[4:8, 0:32] = row_old[...]

    pl.semaphore_wait(barrier, 13)

    tiles = begin([to_cols(i, mine, mine, s_tile.at[i], r_tile.at[i]) for i in range(7)])
    sent = list(tiles)

    def columns(i):
        tx, tc = col_peer(i)
        return pl.ds(pl.multiple_of((tx * 2 + tc) * COLS, 128), COLS)

    grad_copies = begin(
        [to_cols(i, grads.at[:, :, columns(i)], g_out.at[k], s_grad.at[i], r_grad.at[i]) for i in range(7)]
    )
    sent += grad_copies

    def peer_block(i):
        tx, tc = col_peer(i)
        return tx * 2 + tc

    def send_params(m):
        if CODED:
            copies = [
                to_cols(i, qv.at[peer_block(i), m], p_out.at[k, m], s_par.at[m, i], r_par.at[m, i])
                for i in range(7)
            ]
        else:
            copies = [
                to_cols(i, params.at[m, :, columns(i)], p_out.at[k, m], s_par.at[m, i], r_par.at[m, i])
                for i in range(7)
            ]
        begin(copies)
        sent.extend(copies)
        return copies

    par_copies = []
    if not CODED:
        for m in range(FIRST):
            par_copies += send_params(m)

    own_columns = pl.ds(pl.multiple_of(k * COLS, 128), COLS)
    lane32 = iota((ROWS, 128), 1)
    row_sums = jnp.zeros((ROWS, 128), F32)
    own = []
    for m in range(M):
        loads[m].wait()

        def add_squares(t, acc, m=m):
            g = gv[m, :, pl.ds(pl.multiple_of(t * COLS, 128), COLS)].astype(F32)
            sq = g * g + EPS
            for u in range(COLS // 128):
                acc = acc + sq[:, u * 128 : (u + 1) * 128]
            return acc

        part = lax.fori_loop(0, 8, add_squares, jnp.zeros((ROWS, 128), F32))
        total = jnp.sum(part, axis=1, keepdims=True)
        row_sums = row_sums + jnp.where(lane32 == m, total, 0.0)
        own.append(pltpu.make_async_copy(gv.at[m, :, own_columns], g_out.at[k, m], own_sem.at[m]))
        own[-1].start()

    at8 = iota((8, 128), 0)
    lane8 = iota((8, 128), 1)
    squares = jnp.zeros((8, 128), F32)
    for m in range(M):
        loads[M + m].wait()

        def add_weights(t, acc, m=m):
            w = pv[m, :, pl.ds(pl.multiple_of(t * COLS, 128), COLS)]
            sq = w * w
            tops = [jnp.zeros((8, 128), F32)] * 2
            size = jnp.abs(w)
            for u in range(COLS // 128):
                for v in range(ROWS // 8):
                    acc = acc + sq[v * 8 : (v + 1) * 8, u * 128 : (u + 1) * 128]
                    if CODED:
                        tops[u % 2] = jnp.maximum(tops[u % 2], size[v * 8 : (v + 1) * 8, u * 128 : (u + 1) * 128])
            if CODED:
                top = jnp.concatenate([jnp.max(a, axis=0, keepdims=True) for a in tops], axis=1)
                top = jnp.maximum(top, 1e-30)
                sv[t, m : m + 1, :] = top * (1.0 / TOP)
                per = jnp.concatenate([TOP / top] * (COLS // 256), axis=1)
                qv[t, m] = jnp.round(w * per).astype(jnp.int32).astype(jnp.int16)
            return acc

        part = lax.fori_loop(0, 8, add_weights, jnp.zeros((8, 128), F32))
        total = jnp.sum(jnp.sum(part, axis=1, keepdims=True), axis=0, keepdims=True)
        squares = squares + jnp.where((at8 == m) & (lane8 == ROWS), total, 0.0)
        here = qv.at[k, m] if CODED else pv.at[m, :, own_columns]
        own.append(pltpu.make_async_copy(here, p_out.at[k, m], own_sem.at[M + m]))
        own[-1].start()
    if CODED:
        own.append(pltpu.make_async_copy(sv.at[k], s_out.at[k], own_sem.at[2 * M]))
        own[-1].start()
        par_copies += begin(
            [to_cols(i, sv.at[peer_block(i)], s_out.at[k], s_par.at[M, i], r_par.at[M, i]) for i in range(7)]
        )
        sent.extend(par_copies)
        for m in range(FIRST):
            par_copies += send_params(m)

    arrive(tiles)
    line_at = stored.at[pl.ds(pl.multiple_of((z * 4 + y) * 64, 64), 64)]
    lines = begin([to_line("y", d, line_at, line_at, s_line.at[d - 1], r_line.at[d - 1]) for d in LINE_PEERS])
    sent += lines

    arrive(lines)
    slab_at = stored.at[pl.ds(pl.multiple_of(z * 256, 256), 256)]
    slabs = begin([to_line("z", d, slab_at, slab_at, s_line.at[d + 2], r_line.at[d + 2]) for d in LINE_PEERS])
    sent += slabs
    arrive(slabs)

    at_row = iota((128, 128), 0)
    picked = jnp.zeros((128, 128), F32)
    for m in range(M):
        onehot = jnp.where((at_row == m) & (old_map[m : m + 1, :] == f), 1.0, 0.0)
        picked = picked + jnp.dot(
            onehot, stored[pl.ds(4 + m, 128, stride=8), :], precision=HIGHEST, preferred_element_type=F32
        )
    sel[...] = jnp.zeros((128, COLS), F32)
    sel[0:ROWS, 0:128] = row_sums
    row_sums = jnp.transpose(sel[:, 0:128])[0:8, :]
    row_new = DECAY * picked[0:8, :] + (1.0 - DECAY) * row_sums / FF
    row_new = jnp.where((at8 < M) & (lane8 < ROWS), row_new, 1.0)
    row_tiles[64:128, :] = jnp.ones((64, 128), F32)
    own_tile = row_tiles.at[pl.ds(pl.multiple_of(k * 8, 8), 8)]
    own_tile[...] = jnp.where(lane8 == ROWS, squares, row_new)
    row_copies = begin([to_cols(i, own_tile, own_tile, s_row.at[i], r_row.at[i]) for i in range(7)])
    sent += row_copies

    lane = iota((1, COLS), 1)
    block_of = ((lane.astype(F32) + 0.5) * (1.0 / 80.0)).astype(jnp.int32)
    place_of = lane - 80 * block_of
    at64 = iota((64, 128), 0)
    blocks = jnp.zeros((64, 128), F32)
    for m in range(M):
        wanted = (at64 - 16 * m) + k * 16
        inside = (at64 >= 16 * m) & (at64 < 16 * m + 16)
        onehot = jnp.where(inside & (old_map[m : m + 1, :] == wanted), 1.0, 0.0)
        blocks = blocks + jnp.dot(
            onehot, stored[pl.ds(m, 128, stride=8), :], precision=HIGHEST, preferred_element_type=F32
        )
    sel[0:64, 0:128] = blocks
    spread = jnp.where(iota((128, COLS), 0) == place_of, 1.0, 0.0)
    wide = jnp.dot(sel[0:64, 0:128], spread, precision=HIGHEST, preferred_element_type=F32)
    sel[0:64, :] = wide
    at16 = iota((16, COLS), 0)
    old_cols = [
        jnp.sum(jnp.where(at16 == block_of, sel[m * 16 : (m + 1) * 16, :], 0.0), axis=0, keepdims=True)
        for m in range(M)
    ]
    for m in range(M):
        c_out[m : m + 1, :] = old_cols[m]

    arrive(grad_copies)
    for m in range(M):
        own[m].wait()

    red_y[y, 4:8, :] = jnp.zeros((4, COLS), F32)
    for m in range(M):

        def add_columns(t, acc, m=m):
            g = g_out[t, m].astype(F32)
            sq = g * g + EPS
            for v in range(ROWS // 8):
                acc = acc + sq[v * 8 : (v + 1) * 8, :]
            return acc

        part = lax.fori_loop(0, 8, add_columns, jnp.zeros((8, COLS), F32))
        red_y[y, m : m + 1, :] = jnp.sum(part, axis=0, keepdims=True)

    arrive(row_copies)
    tile_sum = row_tiles[0:8, :]
    for t in range(1, 8):
        tile_sum = tile_sum + row_tiles[t * 8 : (t + 1) * 8, :]
    row_sum = jnp.sum(jnp.where(lane8 < ROWS, tile_sum, 0.0), axis=1, keepdims=True)
    weight_sum = jnp.sum(jnp.where(lane8 == ROWS, tile_sum, 0.0), axis=1, keepdims=True)
    both = jnp.where(lane8 == 0, row_sum, jnp.where(lane8 == 1, weight_sum, 0.0))
    red_y[y, 4:8, 0:128] = both[0:4, :]
    own_row = z * 4 + y
    rows_out[own_row] = row_tiles[0:64, :]

    stage = begin(
        [to_line("y", d, red_y.at[y], red_y.at[y], s_red.at[d - 1], r_red.at[d - 1]) for d in LINE_PEERS]
    )
    own_rows = rows_out.at[pl.ds(own_row, 1)]
    rows_y = begin(
        [to_line("y", d, own_rows, own_rows, s_red.at[d + 5], r_red.at[d + 5]) for d in LINE_PEERS]
    )
    arrive(stage)
    sent += stage + rows_y
    red_z[z] = red_y[0] + red_y[1] + red_y[2] + red_y[3]
    stage = begin(
        [to_line("z", d, red_z.at[z], red_z.at[z], s_red.at[d + 2], r_red.at[d + 2]) for d in LINE_PEERS]
    )
    arrive(rows_y)
    slab_rows = rows_out.at[pl.ds(pl.multiple_of(z * 4, 4), 4)]
    rows_z = begin(
        [to_line("z", d, slab_rows, slab_rows, s_red.at[d + 8], r_red.at[d + 8]) for d in LINE_PEERS]
    )
    arrive(stage)
    sent += stage + rows_z
    total = red_z[0] + red_z[1] + red_z[2] + red_z[3]

    row_mean = [total[4 + m : 5 + m, 0:1] / D for m in range(M)]
    param_scale = [jnp.sqrt(total[4 + m : 5 + m, 1:2] / (D * FF) + 1e-6) for m in range(M)]
    col_new = DECAY * c_out[0:M, :] + (1.0 - DECAY) * total[0:M, :] / D
    sel[0:M, :] = col_new
    piece = lax.min(own_row, COLS // 128 - 1)
    cols_out[own_row, k, 0:M, :] = sel[0:M, pl.ds(pl.multiple_of(piece * 128, 128), 128)]
    sel[0:M, :] = 1.0 / col_new
    new_rows = jnp.transpose(row_tiles[...])[0:ROWS, :]
    rnew[...] = 1.0 / new_rows

    update_sum = jnp.zeros((8, 128), F32)
    for m in range(M):
        inv_col = sel[m : m + 1, :]

        def add_updates(t, acc, m=m, inv_col=inv_col):
            g = g_out[t, m].astype(F32)
            sq = g * g * inv_col
            part = sq[:, 0:128]
            for u in range(1, COLS // 128):
                part = part + sq[:, u * 128 : (u + 1) * 128]
            part = part * jnp.sum(jnp.where(lane32 == t * 8 + m, rnew[...], 0.0), axis=1, keepdims=True)
            for v in range(ROWS // 8):
                acc = acc + part[v * 8 : (v + 1) * 8, :]
            return acc

        part = lax.fori_loop(0, 8, add_updates, jnp.zeros((8, 128), F32))
        update_sum = update_sum + part * row_mean[m]
    cols_out[own_row, k, 4:8, :] = update_sum[0:4, :] + update_sum[4:8, :]
    own_col = cols_out.at[own_row, k]
    sums = begin([to_cols(i, own_col, own_col, s_sc.at[i], r_sc.at[i]) for i in range(7)])
    sent += sums

    for m in range(FIRST, M):
        par_copies += send_params(m)

    arrive(sums)
    update_sum = cols_out[own_row, 0, 4:8, :]
    for t in range(1, 8):
        update_sum = update_sum + cols_out[own_row, t, 4:8, :]
    sc_y[y] = jnp.zeros((8, 128), F32)
    sc_y[y, 0:4, :] = update_sum
    stage = begin(
        [to_line("y", d, sc_y.at[y], sc_y.at[y], s_sc.at[d + 6], r_sc.at[d + 6]) for d in LINE_PEERS]
    )
    own_cols = cols_out.at[pl.ds(own_row, 1)]
    cols_y = begin(
        [to_line("y", d, own_cols, own_cols, s_sc.at[d + 12], r_sc.at[d + 12]) for d in LINE_PEERS]
    )
    arrive(stage)
    sent += stage + cols_y
    sc_z[z] = sc_y[0] + sc_y[1] + sc_y[2] + sc_y[3]
    stage = begin(
        [to_line("z", d, sc_z.at[z], sc_z.at[z], s_sc.at[d + 9], r_sc.at[d + 9]) for d in LINE_PEERS]
    )
    arrive(cols_y)
    slab_cols = cols_out.at[pl.ds(pl.multiple_of(z * 4, 4), 4)]
    cols_z = begin(
        [to_line("z", d, slab_cols, slab_cols, s_sc.at[d + 15], r_sc.at[d + 15]) for d in LINE_PEERS]
    )
    arrive(stage)
    sent += stage + cols_z
    update_sum = sc_z[0] + sc_z[1] + sc_z[2] + sc_z[3]
    update_total = jnp.sum(jnp.sum(update_sum, axis=1, keepdims=True), axis=0, keepdims=True)
    clip = jnp.maximum(1.0, jnp.sqrt(update_total / (M * D * FF)))
    factor = jnp.zeros((1, 128), F32)
    for m in range(M):
        own_factor = -(RATE * param_scale[m]) / clip * jnp.sqrt(row_mean[m])
        factor = factor + jnp.where(lax.rem(iota((1, 128), 1), 8) == m, own_factor, 0.0)
    r_out[...] = factor * jnp.sqrt(rnew[...])
    c_out[0:M, :] = jnp.sqrt(sel[0:M, :])

    arrive(rows_z)
    arrive(cols_z)
    for cp in own[M:]:
        cp.wait()
    arrive(par_copies)
    for cp in sent:
        cp.wait_send()


def apply_kernel(
    quarter, p_ref, s_ref, g_ref, r_ref, c_ref, rows_ref, cols_ref, map_ref,
    new_ref, change_ref, row_ref, col_ref,
):
    i = pl.program_id(0)
    m = i // quarter
    at = lax.rem(i, quarter)
    slots = 8 // quarter

    @pl.when(i == 0)
    def _():
        f = lax.axis_index(AXES)
        for n in range(M):
            b = map_ref[n, f]
            row_ref[n : n + 1, :] = rows_ref[b // 8, pl.ds(lax.rem(b, 8) * 8 + n, 1), 0:32]
            start = lax.rem(b, 16) * 80
            first = start // 128
            after = lax.min(first + 1, COLS // 128 - 1)
            pair = [cols_ref[a, b // 16, n : n + 1, :] for a in (first, after)]
            pair = jnp.broadcast_to(jnp.concatenate(pair, axis=1), (8, 256))
            take = jnp.where(iota((256, 128), 0) == start - first * 128 + iota((256, 128), 1), 1.0, 0.0)
            got = jnp.dot(pair, take, precision=HIGHEST, preferred_element_type=F32)
            col_ref[n : n + 1, :] = got[0:1, 0:80]

    lane = iota((ROWS, 128), 1)
    by_col = c_ref[pl.ds(m, 1), :]
    for s in range(slots):
        t = at * slots + s
        by_row = jnp.sum(jnp.where(lane == t * 8 + m, r_ref[...], 0.0), axis=1, keepdims=True)
        g = g_ref[t, m].astype(F32)
        change = (g * by_row) * by_col
        change_ref[0, s * ROWS : (s + 1) * ROWS, :] = change
        if CODED:
            step = s_ref[t, pl.ds(m, 1), :]
            step = jnp.concatenate([step] * (COLS // 256), axis=1)
            weights = p_ref[t, m].astype(jnp.int32).astype(F32) * step
        else:
            weights = p_ref[t, m]
        new_ref[0, s * ROWS : (s + 1) * ROWS, :] = weights + change


def shards(params, grads, row_state_old, col_state_old, old_map, new_map):
    vmem = pl.BlockSpec(memory_space=pltpu.VMEM)
    hbm = pl.BlockSpec(memory_space=pltpu.HBM)
    dma = pltpu.SemaphoreType.DMA
    given = (params, grads, row_state_old, col_state_old, old_map)
    held = [pltpu.with_memory_space_constraint(a, pltpu.HBM) for a in given]
    moved = pl.pallas_call(
        exchange_kernel,
        out_shape=[
            pltpu.VMEM((8, M, ROWS, COLS), jnp.int16 if CODED else F32),
            pltpu.VMEM((8, M, 256), F32),
            pltpu.VMEM((8, M, ROWS, COLS), jnp.bfloat16),
            pltpu.VMEM((ROWS, 128), F32),
            pltpu.VMEM((8, COLS), F32),
            pltpu.VMEM((16, 64, 128), F32),
            pltpu.VMEM((16, 8, 8, 128), F32),
        ],
        in_specs=[hbm] * 5,
        out_specs=[vmem] * 7,
        scratch_shapes=[
            pltpu.VMEM((M, ROWS, FF), jnp.bfloat16),
            pltpu.VMEM((M, ROWS, FF), F32),
            pltpu.VMEM((8, M, ROWS, COLS) if CODED else (8, M, 16, 128), jnp.int16),
            pltpu.VMEM((8, M, 256), F32),
            pltpu.VMEM((M, 32), F32),
            pltpu.VMEM((M, 80), F32),
            pltpu.VMEM((M, 128), jnp.int32),
            pltpu.VMEM((1024, 128), F32),
            pltpu.VMEM((128, 128), F32),
            pltpu.VMEM((4, 8, COLS), F32),
            pltpu.VMEM((4, 8, COLS), F32),
            pltpu.VMEM((4, 8, 128), F32),
            pltpu.VMEM((4, 8, 128), F32),
            pltpu.VMEM((128, COLS), F32),
            pltpu.VMEM((ROWS, 128), F32),
            dma((2 * M,)),
            dma((3,)),
            dma((2 * M + 1,)),
            dma((7,)), dma((7,)),
            dma((6,)), dma((6,)),
            dma((7,)), dma((7,)),
            dma((M + 1, 7)), dma((M + 1, 7)),
            dma((7,)), dma((7,)),
            dma((12,)), dma((12,)),
            dma((19,)), dma((19,)),
        ],
        compiler_params=pltpu.CompilerParams(
            collective_id=0, has_side_effects=True, vmem_limit_bytes=28 << 20
        ),
        name="exchange",
    )(*held)
    quarter = 4
    rows = 256 // quarter
    whole = pl.BlockSpec((1, rows, COLS), lambda i: (i // quarter, lax.rem(i, quarter), 0))
    return pl.pallas_call(
        functools.partial(apply_kernel, quarter),
        grid=(M * quarter,),
        out_shape=[
            jax.ShapeDtypeStruct((M, 256, COLS), F32),
            jax.ShapeDtypeStruct((M, 256, COLS), F32),
            jax.ShapeDtypeStruct((M, 32), F32),
            jax.ShapeDtypeStruct((M, 80), F32),
        ],
        in_specs=[vmem] * 7 + [pl.BlockSpec(memory_space=pltpu.SMEM)],
        out_specs=[
            whole,
            whole,
            pl.BlockSpec((M, 32), lambda i: (0, 0)),
            pl.BlockSpec((M, 80), lambda i: (0, 0)),
        ],
        compiler_params=pltpu.CompilerParams(vmem_limit_bytes=28 << 20),
        name="apply",
    )(*(pltpu.with_memory_space_constraint(a, pltpu.VMEM) for a in moved), new_map)


def solution(mesh):
    torus = Mesh(mesh.devices.reshape(4, 4, 4, 2), AXES)
    over = ("z", "y", "x", "c")
    return jax.shard_map(
        shards,
        mesh=torus,
        in_specs=(P(None, over, None), P(None, over, None), P(None, over), P(None, over), P(), P()),
        out_specs=(
            P(None, ("z", "y"), ("x", "c")),
            P(None, ("z", "y"), ("x", "c")),
            P(None, over),
            P(None, over),
        ),
        check_vma=False,
    )
```

time: 131 us -> 120 us (0.916)
  Pallas kernels: 130 us -> 120 us
    pallas_call x1, Pallas kernels: 117 us -> 111 us  [shards(): pl.pallas_call(exchange_kernel, out_shape=[pltpu.VMEM((8, M, ROWS, COLS),...]
    pallas_call x1, Pallas kernels: 12.9 us -> 8.94 us  [shards(): pl.pallas_call(functools.partial(apply_kernel, quarter), grid=(M * quarte...]
where the time goes in v2:
time: 120 us
  Pallas kernels  120 us (100%)
    pallas_call x1, Pallas kernels, shards(): pl.pallas_call(exchange_kernel, out_shape=[pltpu.VMEM((8, M, ROWS, COLS),...  111 us
    pallas_call x1, Pallas kernels, shards(): pl.pallas_call(functools.partial(apply_kernel, quarter), grid=(M * quarte...  8.94 us

profile of v2, /device:TPU:1, one launch (start us, length us, event | category | flops | bytes accessed | tf_op | source)
XLA Modules:
  0.0 120.2 jit_solution(8880912666970852448)
XLA Ops:
  0.6 0.0 copy-start
  0.6 110.6 %exchange.1 = (f32[8,4,32,1280]{3,2,1,0:T(8,128)S(1)}, f32[8,4,256]{2,1,0:T(4,128)S(1)}, bf16[8,4,32,1280]{3,2,1,0:T(8,128)(2,1)S(1)}, f32[32,128]{1,0:T(8,128)S...) custom-call(f32[4,32,10240]{2,1,0:T(8,128)} %params.1, ...), custom_call_target="tpu_custom_call" | custom-call | tf_op jit(solution)/shard_map/exchange/pallas_call | solution.py:432
  111.3 0.0 copy-done
  111.3 8.9 %apply.1 = (f32[4,256,1280]{2,1,0:T(8,128)}, f32[4,256,1280]{2,1,0:T(8,128)}, f32[4,32]{1,0:T(4,128)}, f32[4,80]{1,0:T(4,128)}) custom-call(f32[8,4,32,1280]{3,2,1,0:T(8,128)S(1)} %get-tuple-element.11.p_ref, f32[8,4,256]{2,1,0:T(4,128)S(1)} %get-tuple-element.12.s_ref, bf16[8,4,32,1280]{3,2,1,0:T(8,128)(2,1)S(1)} %get-tuple-element.13.g_ref, ...), custom_call_target="tpu_custom_call" | custom-call | tf_op jit(solution)/shard_map/apply/pallas_call | solution.py:480
Async XLA Ops:
  0.6 110.6 %copy-start = (s32[4,128]{1,0:T(4,128)S(1)}, s32[4,128]{1,0:T(4,128)}, u32[]{:S(2)}) copy-start(s32[4,128]{1,0:T(4,128)} %map_ref.1) | copy-start | bytes 6148

commit v3 on v2

--- a/solution.py
+++ b/solution.py
@@ -23,7 +23,7 @@
 EPS = 1e-30
 F32 = jnp.float32
 TOP = 32767.0
-CODED = False
+CODED = True
 FIRST = 2
 
 COL_PEERS = [(1, 0), (3, 0), (2, 0), (1, 1), (3, 1), (2, 1), (0, 1)]

time: 120 us -> 93.2 us (0.78)
  Pallas kernels: 120 us -> 92.4 us
    pallas_call x1, Pallas kernels: 111 us -> 83.5 us  [shards(): pl.pallas_call(exchange_kernel, out_shape=[pltpu.VMEM((8, M, ROWS, COLS),...]
where the time goes in v3:
time: 93.2 us; the launch traced here: 93.1 us
  Pallas kernels  92.4 us (99%)
    pallas_call x1, Pallas kernels, shards(): pl.pallas_call(exchange_kernel, out_shape=[pltpu.VMEM((8, M, ROWS, COLS),...  83.5 us
    pallas_call x1, Pallas kernels, shards(): pl.pallas_call(functools.partial(apply_kernel, quarter), grid=(M * quarte...  8.94 us

profile of v3, /device:TPU:1, one launch (start us, length us, event | category | flops | bytes accessed | tf_op | source)
XLA Modules:
  0.0 93.1 jit_solution(8467286932470388102)
XLA Ops:
  0.6 0.0 copy-start
  0.6 83.5 %exchange.1 = (s16[8,4,32,1280]{3,2,1,0:T(8,128)(2,1)S(1)}, f32[8,4,256]{2,1,0:T(4,128)S(1)}, bf16[8,4,32,1280]{3,2,1,0:T(8,128)(2,1)S(1)}, f32[32,128]{1,0:T(8,...) custom-call(f32[4,32,10240]{2,1,0:T(8,128)} %params.1, ...), custom_call_target="tpu_custom_call" | custom-call | tf_op jit(solution)/shard_map/exchange/pallas_call | solution.py:432
  84.2 0.0 copy-done
  84.2 8.9 %apply.1 = (f32[4,256,1280]{2,1,0:T(8,128)}, f32[4,256,1280]{2,1,0:T(8,128)}, f32[4,32]{1,0:T(4,128)}, f32[4,80]{1,0:T(4,128)}) custom-call(s16[8,4,32,1280]{3,2,1,0:T(8,128)(2,1)S(1)} %get-tuple-element.11.p_ref, f32[8,4,256]{2,1,0:T(4,128)S(1)} %get-tuple-element.12.s_ref, bf16[8,4,32,1280]{3,2,1,0:T(8,128)(2,1)S(1)} %get-tuple-element.13.g_ref, ...), custom_call_target="tpu_custom_call" | custom-call | tf_op jit(solution)/shard_map/apply/pallas_call | solution.py:480
Async XLA Ops:
  0.6 83.5 %copy-start = (s32[4,128]{1,0:T(4,128)S(1)}, s32[4,128]{1,0:T(4,128)}, u32[]{:S(2)}) copy-start(s32[4,128]{1,0:T(4,128)} %map_ref.1) | copy-start | bytes 6148

commit v4 on v3

--- a/solution.py
+++ b/solution.py
@@ -1,4 +1,3 @@
-import functools
 import math
 
 import jax
@@ -24,6 +23,7 @@
 F32 = jnp.float32
 TOP = 32767.0
 CODED = True
+PIECE = 3
 FIRST = 2
 
 COL_PEERS = [(1, 0), (3, 0), (2, 0), (1, 1), (3, 1), (2, 1), (0, 1)]
@@ -37,10 +37,10 @@
 def exchange_kernel(
     params, grads, row_hbm, col_hbm, map_hbm,
     p_out, s_out, g_out, r_out, c_out, rows_out, cols_out,
-    gv, pv, qv, sv, row_old, col_old, old_map, stored, row_tiles, red_y, red_z, sc_y, sc_z, sel, rnew,
+    gv, pv, qv, sv, row_old, col_old, old_map, stored, row_tiles, red_y, red_z, sc_x, sc_y, sc_z, sel, rnew,
     load_sem, small_sem, own_sem,
     s_tile, r_tile, s_line, r_line, s_grad, r_grad, s_par, r_par,
-    s_row, r_row, s_red, r_red, s_sc, r_sc,
+    s_row, r_row, s_red, r_red, s_sc, r_sc, s_col, r_col,
 ):
     z, y, x, c = (lax.axis_index(a) for a in AXES)
     k = x * 2 + c
@@ -135,9 +135,6 @@
         return copies
 
     par_copies = []
-    if not CODED:
-        for m in range(FIRST):
-            par_copies += send_params(m)
 
     own_columns = pl.ds(pl.multiple_of(k * COLS, 128), COLS)
     lane32 = iota((ROWS, 128), 1)
@@ -196,8 +193,6 @@
             [to_cols(i, sv.at[peer_block(i)], s_out.at[k], s_par.at[M, i], r_par.at[M, i]) for i in range(7)]
         )
         sent.extend(par_copies)
-        for m in range(FIRST):
-            par_copies += send_params(m)
 
     arrive(tiles)
     line_at = stored.at[pl.ds(pl.multiple_of((z * 4 + y) * 64, 64), 64)]
@@ -227,6 +222,8 @@
     own_tile[...] = jnp.where(lane8 == ROWS, squares, row_new)
     row_copies = begin([to_cols(i, own_tile, own_tile, s_row.at[i], r_row.at[i]) for i in range(7)])
     sent += row_copies
+    for m in range(FIRST):
+        par_copies += send_params(m)
 
     lane = iota((1, COLS), 1)
     block_of = ((lane.astype(F32) + 0.5) * (1.0 / 80.0)).astype(jnp.int32)
@@ -306,8 +303,8 @@
     param_scale = [jnp.sqrt(total[4 + m : 5 + m, 1:2] / (D * FF) + 1e-6) for m in range(M)]
     col_new = DECAY * c_out[0:M, :] + (1.0 - DECAY) * total[0:M, :] / D
     sel[0:M, :] = col_new
-    piece = lax.min(own_row, COLS // 128 - 1)
-    cols_out[own_row, k, 0:M, :] = sel[0:M, pl.ds(pl.multiple_of(piece * 128, 128), 128)]
+    piece = lax.min(y * PIECE, COLS // 128 - PIECE)
+    cols_out[y, k] = sel[0:M, pl.ds(pl.multiple_of(piece * 128, 128), PIECE * 128)]
     sel[0:M, :] = 1.0 / col_new
     new_rows = jnp.transpose(row_tiles[...])[0:ROWS, :]
     rnew[...] = 1.0 / new_rows
@@ -329,26 +326,27 @@
 
         part = lax.fori_loop(0, 8, add_updates, jnp.zeros((8, 128), F32))
         update_sum = update_sum + part * row_mean[m]
-    cols_out[own_row, k, 4:8, :] = update_sum[0:4, :] + update_sum[4:8, :]
-    own_col = cols_out.at[own_row, k]
-    sums = begin([to_cols(i, own_col, own_col, s_sc.at[i], r_sc.at[i]) for i in range(7)])
-    sent += sums
+    sc_x[k] = update_sum
+    sums = begin([to_cols(i, sc_x.at[k], sc_x.at[k], s_sc.at[i], r_sc.at[i]) for i in range(7)])
+    own_col = cols_out.at[y, k]
+    cols_x = begin([to_cols(i, own_col, own_col, s_col.at[i], r_col.at[i]) for i in range(7)])
+    sent += sums + cols_x
 
     for m in range(FIRST, M):
         par_copies += send_params(m)
 
     arrive(sums)
-    update_sum = cols_out[own_row, 0, 4:8, :]
+    update_sum = sc_x[0]
     for t in range(1, 8):
-        update_sum = update_sum + cols_out[own_row, t, 4:8, :]
-    sc_y[y] = jnp.zeros((8, 128), F32)
-    sc_y[y, 0:4, :] = update_sum
+        update_sum = update_sum + sc_x[t]
+    sc_y[y] = update_sum
     stage = begin(
         [to_line("y", d, sc_y.at[y], sc_y.at[y], s_sc.at[d + 6], r_sc.at[d + 6]) for d in LINE_PEERS]
     )
-    own_cols = cols_out.at[pl.ds(own_row, 1)]
+    arrive(cols_x)
+    own_cols = cols_out.at[pl.ds(y, 1)]
     cols_y = begin(
-        [to_line("y", d, own_cols, own_cols, s_sc.at[d + 12], r_sc.at[d + 12]) for d in LINE_PEERS]
+        [to_line("y", d, own_cols, own_cols, s_col.at[d + 6], r_col.at[d + 6]) for d in LINE_PEERS]
     )
     arrive(stage)
     sent += stage + cols_y
@@ -356,13 +354,8 @@
     stage = begin(
         [to_line("z", d, sc_z.at[z], sc_z.at[z], s_sc.at[d + 9], r_sc.at[d + 9]) for d in LINE_PEERS]
     )
-    arrive(cols_y)
-    slab_cols = cols_out.at[pl.ds(pl.multiple_of(z * 4, 4), 4)]
-    cols_z = begin(
-        [to_line("z", d, slab_cols, slab_cols, s_sc.at[d + 15], r_sc.at[d + 15]) for d in LINE_PEERS]
-    )
     arrive(stage)
-    sent += stage + cols_z
+    sent += stage
     update_sum = sc_z[0] + sc_z[1] + sc_z[2] + sc_z[3]
     update_total = jnp.sum(jnp.sum(update_sum, axis=1, keepdims=True), axis=0, keepdims=True)
     clip = jnp.maximum(1.0, jnp.sqrt(update_total / (M * D * FF)))
@@ -374,7 +367,7 @@
     c_out[0:M, :] = jnp.sqrt(sel[0:M, :])
 
     arrive(rows_z)
-    arrive(cols_z)
+    arrive(cols_y)
     for cp in own[M:]:
         cp.wait()
     arrive(par_copies)
@@ -383,44 +376,75 @@
 
 
 def apply_kernel(
-    quarter, p_ref, s_ref, g_ref, r_ref, c_ref, rows_ref, cols_ref, map_ref,
-    new_ref, change_ref, row_ref, col_ref,
+    p_ref, s_ref, g_ref, r_ref, c_ref, rows_ref, cols_ref, map_hbm,
+    new_hbm, change_hbm, row_hbm, col_hbm,
+    new_buf, change_buf, row_buf, col_buf, new_map, big_sem, small_sem,
 ):
-    i = pl.program_id(0)
-    m = i // quarter
-    at = lax.rem(i, quarter)
-    slots = 8 // quarter
-
-    @pl.when(i == 0)
-    def _():
-        f = lax.axis_index(AXES)
-        for n in range(M):
-            b = map_ref[n, f]
-            row_ref[n : n + 1, :] = rows_ref[b // 8, pl.ds(lax.rem(b, 8) * 8 + n, 1), 0:32]
-            start = lax.rem(b, 16) * 80
-            first = start // 128
-            after = lax.min(first + 1, COLS // 128 - 1)
-            pair = [cols_ref[a, b // 16, n : n + 1, :] for a in (first, after)]
-            pair = jnp.broadcast_to(jnp.concatenate(pair, axis=1), (8, 256))
-            take = jnp.where(iota((256, 128), 0) == start - first * 128 + iota((256, 128), 1), 1.0, 0.0)
-            got = jnp.dot(pair, take, precision=HIGHEST, preferred_element_type=F32)
-            col_ref[n : n + 1, :] = got[0:1, 0:80]
-
+    fetch = pltpu.make_async_copy(map_hbm, new_map, small_sem.at[0])
+    fetch.start()
     lane = iota((ROWS, 128), 1)
-    by_col = c_ref[pl.ds(m, 1), :]
-    for s in range(slots):
-        t = at * slots + s
-        by_row = jnp.sum(jnp.where(lane == t * 8 + m, r_ref[...], 0.0), axis=1, keepdims=True)
-        g = g_ref[t, m].astype(F32)
-        change = (g * by_row) * by_col
-        change_ref[0, s * ROWS : (s + 1) * ROWS, :] = change
-        if CODED:
-            step = s_ref[t, pl.ds(m, 1), :]
-            step = jnp.concatenate([step] * (COLS // 256), axis=1)
-            weights = p_ref[t, m].astype(jnp.int32).astype(F32) * step
-        else:
-            weights = p_ref[t, m]
-        new_ref[0, s * ROWS : (s + 1) * ROWS, :] = weights + change
+
+    def stores(m, t):
+        rows = pl.ds(pl.multiple_of(t * ROWS, ROWS), ROWS)
+        return [
+            pltpu.make_async_copy(change_buf.at[m, rows], change_hbm.at[m, rows], big_sem.at[0, m, t]),
+            pltpu.make_async_copy(new_buf.at[m, rows], new_hbm.at[m, rows], big_sem.at[1, m, t]),
+        ]
+
+    for m in range(M):
+        by_col = c_ref[m : m + 1, :]
+
+        def block(t, carry, m=m, by_col=by_col):
+            rows = pl.ds(pl.multiple_of(t * ROWS, ROWS), ROWS)
+            by_row = jnp.sum(jnp.where(lane == t * 8 + m, r_ref[...], 0.0), axis=1, keepdims=True)
+            g = g_ref[t, m].astype(F32)
+            change = (g * by_row) * by_col
+            change_buf[m, rows, :] = change
+            if CODED:
+                step = jnp.concatenate([s_ref[t, m : m + 1, :]] * (COLS // 256), axis=1)
+                weights = p_ref[t, m].astype(jnp.int32).astype(F32) * step
+            else:
+                weights = p_ref[t, m]
+            new_buf[m, rows, :] = weights + change
+            for cp in stores(m, t):
+                cp.start()
+            return carry
+
+        lax.fori_loop(0, 8, block, 0)
+
+    fetch.wait()
+    f = lax.axis_index(AXES)
+    for n in range(M):
+        b = new_map[n, f]
+        row_buf[n : n + 1, :] = rows_ref[b // 8, pl.ds(lax.rem(b, 8) * 8 + n, 1), 0:32]
+        start = lax.rem(b, 16) * 80
+        first = start // 128
+        pair = []
+        for t in (first, lax.min(first + 1, COLS // 128 - 1)):
+            piece = lax.min(t // PIECE, 3)
+            at = t - lax.min(piece * PIECE, COLS // 128 - PIECE)
+            pair.append(cols_ref[piece, b // 16, n : n + 1, pl.ds(pl.multiple_of(at * 128, 128), 128)])
+        pair = jnp.broadcast_to(jnp.concatenate(pair, axis=1), (8, 256))
+        take = jnp.where(iota((256, 128), 0) == start - first * 128 + iota((256, 128), 1), 1.0, 0.0)
+        got = jnp.dot(pair, take, precision=HIGHEST, preferred_element_type=F32)
+        col_buf[n : n + 1, :] = got[0:1, 0:80]
+    small = [
+        pltpu.make_async_copy(row_buf, row_hbm, small_sem.at[1]),
+        pltpu.make_async_copy(col_buf, col_hbm, small_sem.at[2]),
+    ]
+    for cp in small:
+        cp.start()
+
+    for m in range(M):
+
+        def finish(t, carry, m=m):
+            for cp in stores(m, t):
+                cp.wait()
+            return carry
+
+        lax.fori_loop(0, 8, finish, 0)
+    for cp in small:
+        cp.wait()
 
 
 def shards(params, grads, row_state_old, col_state_old, old_map, new_map):
@@ -429,6 +453,7 @@
     dma = pltpu.SemaphoreType.DMA
     given = (params, grads, row_state_old, col_state_old, old_map)
     held = [pltpu.with_memory_space_constraint(a, pltpu.HBM) for a in given]
+    held_map = pltpu.with_memory_space_constraint(new_map, pltpu.HBM)
     moved = pl.pallas_call(
         exchange_kernel,
         out_shape=[
@@ -438,7 +463,7 @@
             pltpu.VMEM((ROWS, 128), F32),
             pltpu.VMEM((8, COLS), F32),
             pltpu.VMEM((16, 64, 128), F32),
-            pltpu.VMEM((16, 8, 8, 128), F32),
+            pltpu.VMEM((4, 8, M, PIECE * 128), F32),
         ],
         in_specs=[hbm] * 5,
         out_specs=[vmem] * 7,
@@ -454,6 +479,7 @@
             pltpu.VMEM((128, 128), F32),
             pltpu.VMEM((4, 8, COLS), F32),
             pltpu.VMEM((4, 8, COLS), F32),
+            pltpu.VMEM((8, 8, 128), F32),
             pltpu.VMEM((4, 8, 128), F32),
             pltpu.VMEM((4, 8, 128), F32),
             pltpu.VMEM((128, COLS), F32),
@@ -467,35 +493,36 @@
             dma((M + 1, 7)), dma((M + 1, 7)),
             dma((7,)), dma((7,)),
             dma((12,)), dma((12,)),
-            dma((19,)), dma((19,)),
+            dma((13,)), dma((13,)),
+            dma((10,)), dma((10,)),
         ],
         compiler_params=pltpu.CompilerParams(
             collective_id=0, has_side_effects=True, vmem_limit_bytes=28 << 20
         ),
         name="exchange",
     )(*held)
-    quarter = 4
-    rows = 256 // quarter
-    whole = pl.BlockSpec((1, rows, COLS), lambda i: (i // quarter, lax.rem(i, quarter), 0))
     return pl.pallas_call(
-        functools.partial(apply_kernel, quarter),
-        grid=(M * quarter,),
+        apply_kernel,
         out_shape=[
             jax.ShapeDtypeStruct((M, 256, COLS), F32),
             jax.ShapeDtypeStruct((M, 256, COLS), F32),
             jax.ShapeDtypeStruct((M, 32), F32),
             jax.ShapeDtypeStruct((M, 80), F32),
         ],
-        in_specs=[vmem] * 7 + [pl.BlockSpec(memory_space=pltpu.SMEM)],
-        out_specs=[
-            whole,
-            whole,
-            pl.BlockSpec((M, 32), lambda i: (0, 0)),
-            pl.BlockSpec((M, 80), lambda i: (0, 0)),
+        in_specs=[vmem] * 7 + [hbm],
+        out_specs=[hbm] * 4,
+        scratch_shapes=[
+            pltpu.VMEM((M, 256, COLS), F32),
+            pltpu.VMEM((M, 256, COLS), F32),
+            pltpu.VMEM((M, 32), F32),
+            pltpu.VMEM((M, 80), F32),
+            pltpu.SMEM((M, 128), jnp.int32),
+            dma((2, M, 8)),
+            dma((3,)),
         ],
         compiler_params=pltpu.CompilerParams(vmem_limit_bytes=28 << 20),
         name="apply",
-    )(*(pltpu.with_memory_space_constraint(a, pltpu.VMEM) for a in moved), new_map)
+    )(*(pltpu.with_memory_space_constraint(a, pltpu.VMEM) for a in moved), held_map)
 
 
 def solution(mesh):

time: 93.2 us -> 76.2 us (0.82)
  Pallas kernels: 92.4 us -> 75.4 us
    pallas_call x1, Pallas kernels: 83.5 us -> 70.6 us  [shards(): pl.pallas_call(exchange_kernel, out_shape=[pltpu.VMEM((8, M, ROWS, COLS),...]
    pallas_call x1, Pallas kernels: 8.94 us -> 4.88 us  [shards(): pl.pallas_call(apply_kernel, out_shape=[jax.ShapeDtypeStruct((M, 256, COL...]
where the time goes in v4:
time: 76.2 us; the launch traced here: 76.1 us
  Pallas kernels  75.4 us (99%)
    pallas_call x1, Pallas kernels, shards(): pl.pallas_call(exchange_kernel, out_shape=[pltpu.VMEM((8, M, ROWS, COLS),...  70.6 us
    pallas_call x1, Pallas kernels, shards(): pl.pallas_call(apply_kernel, out_shape=[jax.ShapeDtypeStruct((M, 256, COL...  4.88 us

profile of v4, /device:TPU:1, one launch (start us, length us, event | category | flops | bytes accessed | tf_op | source)
XLA Modules:
  0.0 76.1 jit_solution(11938093703247638818)
XLA Ops:
  0.6 70.6 %exchange.1 = (s16[8,4,32,1280]{3,2,1,0:T(8,128)(2,1)S(1)}, f32[8,4,256]{2,1,0:T(4,128)S(1)}, bf16[8,4,32,1280]{3,2,1,0:T(8,128)(2,1)S(1)}, f32[32,128]{1,0:T(8,...) custom-call(f32[4,32,10240]{2,1,0:T(8,128)} %params.1, ...), custom_call_target="tpu_custom_call" | custom-call | tf_op jit(solution)/shard_map/exchange/pallas_call | solution.py:457
  71.2 4.9 %apply.1 = (f32[4,256,1280]{2,1,0:T(8,128)}, f32[4,256,1280]{2,1,0:T(8,128)}, f32[4,32]{1,0:T(4,128)}, f32[4,80]{1,0:T(4,128)}) custom-call(s16[8,4,32,1280]{3,2,1,0:T(8,128)(2,1)S(1)} %get-tuple-element.11.p_ref, f32[8,4,256]{2,1,0:T(4,128)S(1)} %get-tuple-element.12.s_ref, bf16[8,4,32,1280]{3,2,1,0:T(8,128)(2,1)S(1)} %get-tuple-element.13.g_ref, ...), custom_call_target="tpu_custom_call" | custom-call | tf_op jit(solution)/shard_map/apply/pallas_call | solution.py:504

commit v5 on v4

v5 whole, which is shorter than its diff:
```python
import math

import jax
import jax.numpy as jnp
from jax import lax
from jax.experimental import pallas as pl
from jax.experimental.pallas import tpu as pltpu
from jax.sharding import Mesh
from jax.sharding import PartitionSpec as P

D = 4096
FF = 10240
STEP = 4
M = 4
ROWS = 32
COLS = 1280
AXES = ("z", "y", "x", "c")
MESH = pl.DeviceIdType.MESH
HIGHEST = lax.Precision.HIGHEST
DECAY = 1.0 - float(STEP) ** (-0.8)
RATE = min(0.01, 1.0 / math.sqrt(STEP))
EPS = 1e-30
F32 = jnp.float32
TOP = 32767.0
PIECE = 3
PARTS = [(0, 0, 32), (1, 0, 32), (2, 0, 16), (2, 16, 16), (3, 0, 32)]
FIRST = 3

COL_PEERS = [(1, 0), (3, 0), (2, 0), (1, 1), (3, 1), (2, 1), (0, 1)]
LINE_PEERS = [1, 2, 3]


def iota(shape, dim):
    return lax.broadcasted_iota(jnp.int32, shape, dim)


def decoded(codes, steps, t, m):
    step = jnp.concatenate([steps[t, m : m + 1, :]] * (COLS // 256), axis=1)
    return codes[t, m].astype(jnp.int32).astype(F32) * step


def exchange_kernel(
    params, grads, row_hbm, col_hbm, map_hbm,
    new_out, change_out, p_out, s_out, rows_out, cols_out,
    g_in, by_row, by_col, gv, pv, qv, sv, row_old, col_old, old_map, stored, row_tiles, red_y, red_z, two_y, two_z, sc_x, sel, rnew,
    load_sem, small_sem, own_sem,
    s_tile, r_tile, s_line, r_line, s_grad, r_grad, s_par, r_par,
    s_row, r_row, s_red, r_red, s_sc, r_sc, s_col, r_col,
):
    z, y, x, c = (lax.axis_index(a) for a in AXES)
    k = x * 2 + c
    f = (z * 4 + y) * 8 + k

    def col_peer(i):
        dx, dc = COL_PEERS[i]
        return lax.rem(x + dx, 4), lax.rem(c + dc, 2)

    def to_cols(i, src, dst, ss, rs):
        tx, tc = col_peer(i)
        return pltpu.make_async_remote_copy(
            src_ref=src, dst_ref=dst, send_sem=ss, recv_sem=rs,
            device_id={"x": tx, "c": tc}, device_id_type=MESH,
        )

    def to_line(axis, d, src, dst, ss, rs):
        at = lax.rem((y if axis == "y" else z) + d, 4)
        return pltpu.make_async_remote_copy(
            src_ref=src, dst_ref=dst, send_sem=ss, recv_sem=rs,
            device_id={axis: at}, device_id_type=MESH,
        )

    def begin(copies):
        for cp in copies:
            cp.start()
        return copies

    def arrive(copies):
        for cp in copies:
            cp.wait_recv()

    barrier = pltpu.get_barrier_semaphore()
    for i in range(7):
        tx, tc = col_peer(i)
        pl.semaphore_signal(barrier, inc=1, device_id={"x": tx, "c": tc}, device_id_type=MESH)
    for d in LINE_PEERS:
        pl.semaphore_signal(barrier, inc=1, device_id={"y": lax.rem(y + d, 4)}, device_id_type=MESH)
        pl.semaphore_signal(barrier, inc=1, device_id={"z": lax.rem(z + d, 4)}, device_id_type=MESH)

    small = [
        pltpu.make_async_copy(row_hbm, row_old, small_sem.at[0]),
        pltpu.make_async_copy(col_hbm, col_old, small_sem.at[1]),
        pltpu.make_async_copy(map_hbm, old_map, small_sem.at[2]),
    ]
    begin(small)
    loads = []
    for m in range(M):
        loads.append(pltpu.make_async_copy(grads.at[m], gv.at[m], load_sem.at[m]))
    for m in range(M):
        loads.append(pltpu.make_async_copy(params.at[m], pv.at[m], load_sem.at[M + m]))
    begin(loads)

    pl.semaphore_wait(barrier, 13)

    def columns(i):
        tx, tc = col_peer(i)
        return pl.ds(pl.multiple_of((tx * 2 + tc) * COLS, 128), COLS)

    def send_grads(first, count, n):
        part = pl.ds(first, count)
        copies = [
            to_cols(i, grads.at[part, :, columns(i)], g_in.at[k, part], s_grad.at[n, i], r_grad.at[n, i])
            for i in range(7)
        ]
        return begin(copies)

    grad_copies = send_grads(0, 1, 0)

    mine = stored.at[pl.ds(pl.multiple_of(f * 8, 8), 8)]
    mine[...] = jnp.zeros((8, 128), F32)
    for cp in small:
        cp.wait()
    mine[0:4, 0:80] = col_old[...]
    mine[4:8, 0:32] = row_old[...]

    tiles = begin([to_cols(i, mine, mine, s_tile.at[i], r_tile.at[i]) for i in range(7)])
    grad_copies += send_grads(1, M - 1, 1)
    sent = tiles + grad_copies

    def peer_block(i):
        tx, tc = col_peer(i)
        return tx * 2 + tc

    def send_params(n):
        m, first, count = PARTS[n]
        rows = pl.ds(first, count)
        copies = begin(
            [
                to_cols(i, qv.at[peer_block(i), m, rows], p_out.at[k, m, rows], s_par.at[n, i], r_par.at[n, i])
                for i in range(7)
            ]
        )
        sent.extend(copies)
        return copies

    par_copies = []
    own_columns = pl.ds(pl.multiple_of(k * COLS, 128), COLS)
    lane32 = iota((ROWS, 128), 1)
    row_sums = jnp.zeros((ROWS, 128), F32)
    own = []
    for m in range(M):
        loads[m].wait()

        def add_squares(t, acc, m=m):
            g = gv[m, :, pl.ds(pl.multiple_of(t * COLS, 128), COLS)].astype(F32)
            sq = g * g + EPS
            for u in range(COLS // 128):
                acc = acc + sq[:, u * 128 : (u + 1) * 128]
            return acc

        part = lax.fori_loop(0, 8, add_squares, jnp.zeros((ROWS, 128), F32))
        total = jnp.sum(part, axis=1, keepdims=True)
        row_sums = row_sums + jnp.where(lane32 == m, total, 0.0)
        own.append(pltpu.make_async_copy(gv.at[m, :, own_columns], g_in.at[k, m], own_sem.at[m]))
        own[-1].start()

    at8 = iota((8, 128), 0)
    lane8 = iota((8, 128), 1)
    squares = jnp.zeros((8, 128), F32)
    for m in range(M):
        loads[M + m].wait()

        def add_weights(t, acc, m=m):
            w = pv[m, :, pl.ds(pl.multiple_of(t * COLS, 128), COLS)]
            sq = w * w
            tops = [jnp.zeros((8, 128), F32)] * 2
            size = jnp.abs(w)
            for u in range(COLS // 128):
                for v in range(ROWS // 8):
                    acc = acc + sq[v * 8 : (v + 1) * 8, u * 128 : (u + 1) * 128]
                    tops[u % 2] = jnp.maximum(tops[u % 2], size[v * 8 : (v + 1) * 8, u * 128 : (u + 1) * 128])
            top = jnp.concatenate([jnp.max(a, axis=0, keepdims=True) for a in tops], axis=1)
            top = jnp.maximum(top, 1e-30)
            sv[t, m : m + 1, :] = top * (1.0 / TOP)
            per = jnp.concatenate([TOP / top] * (COLS // 256), axis=1)
            qv[t, m] = jnp.round(w * per).astype(jnp.int32).astype(jnp.int16)
            return acc

        part = lax.fori_loop(0, 8, add_weights, jnp.zeros((8, 128), F32))
        total = jnp.sum(jnp.sum(part, axis=1, keepdims=True), axis=0, keepdims=True)
        squares = squares + jnp.where((at8 == m) & (lane8 == ROWS), total, 0.0)
        own.append(pltpu.make_async_copy(qv.at[k, m], p_out.at[k, m], own_sem.at[M + m]))
        own[-1].start()
    own.append(pltpu.make_async_copy(sv.at[k], s_out.at[k], own_sem.at[2 * M]))
    own[-1].start()
    steps = begin([to_cols(i, sv.at[peer_block(i)], s_out.at[k], s_par.at[len(PARTS), i], r_par.at[len(PARTS), i]) for i in range(7)])
    sent += steps

    arrive(tiles)
    line_at = stored.at[pl.ds(pl.multiple_of((z * 4 + y) * 64, 64), 64)]
    lines = begin([to_line("y", d, line_at, line_at, s_line.at[d - 1], r_line.at[d - 1]) for d in LINE_PEERS])
    sent += lines

    arrive(lines)
    slab_at = stored.at[pl.ds(pl.multiple_of(z * 256, 256), 256)]
    slabs = begin([to_line("z", d, slab_at, slab_at, s_line.at[d + 2], r_line.at[d + 2]) for d in LINE_PEERS])
    sent += slabs
    arrive(slabs)

    at_row = iota((128, 128), 0)
    picked = jnp.zeros((128, 128), F32)
    for m in range(M):
        onehot = jnp.where((at_row == m) & (old_map[m : m + 1, :] == f), 1.0, 0.0)
        picked = picked + jnp.dot(
            onehot, stored[pl.ds(4 + m, 128, stride=8), :], precision=HIGHEST, preferred_element_type=F32
        )
    sel[...] = jnp.zeros((128, COLS), F32)
    sel[0:ROWS, 0:128] = row_sums
    row_sums = jnp.transpose(sel[:, 0:128])[0:8, :]
    row_new = DECAY * picked[0:8, :] + (1.0 - DECAY) * row_sums / FF
    row_new = jnp.where((at8 < M) & (lane8 < ROWS), row_new, 1.0)
    own_tile = row_tiles.at[k]
    own_tile[...] = jnp.where(lane8 == ROWS, squares, row_new)[0:M, :]
    row_copies = begin([to_cols(i, own_tile, own_tile, s_row.at[i], r_row.at[i]) for i in range(7)])
    sent += row_copies
    for n in range(FIRST):
        par_copies.append(send_params(n))

    lane = iota((1, COLS), 1)
    block_of = ((lane.astype(F32) + 0.5) * (1.0 / 80.0)).astype(jnp.int32)
    place_of = lane - 80 * block_of
    at64 = iota((64, 128), 0)
    blocks = jnp.zeros((64, 128), F32)
    for m in range(M):
        wanted = (at64 - 16 * m) + k * 16
        inside = (at64 >= 16 * m) & (at64 < 16 * m + 16)
        onehot = jnp.where(inside & (old_map[m : m + 1, :] == wanted), 1.0, 0.0)
        blocks = blocks + jnp.dot(
            onehot, stored[pl.ds(m, 128, stride=8), :], precision=HIGHEST, preferred_element_type=F32
        )
    sel[0:64, 0:128] = blocks
    spread = jnp.where(iota((128, COLS), 0) == place_of, 1.0, 0.0)
    wide = jnp.dot(sel[0:64, 0:128], spread, precision=HIGHEST, preferred_element_type=F32)
    sel[0:64, :] = wide
    at16 = iota((16, COLS), 0)
    old_cols = [
        jnp.sum(jnp.where(at16 == block_of, sel[m * 16 : (m + 1) * 16, :], 0.0), axis=0, keepdims=True)
        for m in range(M)
    ]
    for m in range(M):
        by_col[m : m + 1, :] = old_cols[m]

    arrive(grad_copies)
    for m in range(M):
        own[m].wait()
    arrive(row_copies)
    tile_sum = row_tiles[0]
    for t in range(1, 8):
        tile_sum = tile_sum + row_tiles[t]
    lane4 = iota((M, 128), 1)
    row_sum = jnp.sum(jnp.where(lane4 < ROWS, tile_sum, 0.0), axis=1, keepdims=True)
    weight_sum = jnp.sum(jnp.where(lane4 == ROWS, tile_sum, 0.0), axis=1, keepdims=True)
    two_y[y] = jnp.where(lane4 == 0, row_sum, jnp.where(lane4 == 1, weight_sum, 0.0))
    own_row = z * 4 + y
    rows_out[own_row] = row_tiles[...]
    sel[:, 128:256] = jnp.ones((128, 128), F32)
    for t in range(8):
        sel[t * 8 : t * 8 + M, 128:256] = row_tiles[t]
    rnew[...] = 1.0 / jnp.transpose(sel[:, 128:256])[0:ROWS, :]

    for m in range(M):

        def add_columns(t, sums, m=m):
            plain, scaled = sums
            row = jnp.sum(jnp.where(lane32 == t * 8 + m, rnew[...], 0.0), axis=1, keepdims=True)
            g = g_in[t, m].astype(F32)
            sq = g * g
            by_rows = sq * row
            sq = sq + EPS
            for v in range(ROWS // 8):
                plain = plain + sq[v * 8 : (v + 1) * 8, :]
                scaled = scaled + by_rows[v * 8 : (v + 1) * 8, :]
            return plain, scaled

        nothing = jnp.zeros((8, COLS), F32)
        plain, scaled = lax.fori_loop(0, 8, add_columns, (nothing, nothing))
        red_y[y, m : m + 1, :] = jnp.sum(plain, axis=0, keepdims=True)
        red_y[y, M + m : M + m + 1, :] = jnp.sum(scaled, axis=0, keepdims=True)

    def reduce_over(axis, at, big, little, n):
        copies = []
        for d in LINE_PEERS:
            copies.append(to_line(axis, d, little.at[at], little.at[at], s_red.at[n + d - 1], r_red.at[n + d - 1]))
            copies.append(to_line(axis, d, big.at[at], big.at[at], s_red.at[n + d + 2], r_red.at[n + d + 2]))
        return begin(copies)

    stage = reduce_over("y", y, red_y, two_y, 0)
    own_rows = rows_out.at[pl.ds(own_row, 1)]
    rows_y = begin(
        [to_line("y", d, own_rows, own_rows, s_red.at[d + 11], r_red.at[d + 11]) for d in LINE_PEERS]
    )
    arrive(stage)
    sent += stage + rows_y
    red_z[z] = red_y[0] + red_y[1] + red_y[2] + red_y[3]
    two_z[z] = two_y[0] + two_y[1] + two_y[2] + two_y[3]
    stage = reduce_over("z", z, red_z, two_z, 6)
    arrive(rows_y)
    slab_rows = rows_out.at[pl.ds(pl.multiple_of(z * 4, 4), 4)]
    rows_z = begin(
        [to_line("z", d, slab_rows, slab_rows, s_red.at[d + 14], r_red.at[d + 14]) for d in LINE_PEERS]
    )
    arrive(stage)
    sent += stage + rows_z
    total = red_z[0] + red_z[1] + red_z[2] + red_z[3]
    two = two_z[0] + two_z[1] + two_z[2] + two_z[3]

    row_mean = two[:, 0:1] / D
    param_scale = jnp.sqrt(two[:, 1:2] / (D * FF) + 1e-6)
    col_new = DECAY * by_col[0:M, :] + (1.0 - DECAY) * total[0:M, :] / D
    sel[0:M, :] = col_new
    piece = lax.min(y * PIECE, COLS // 128 - PIECE)
    cols_out[y, k] = sel[0:M, pl.ds(pl.multiple_of(piece * 128, 128), PIECE * 128)]
    inv_col = 1.0 / col_new

    update_sum = jnp.sum(total[M : 2 * M, :] * inv_col, axis=1, keepdims=True) * row_mean
    sc_x[k] = jnp.broadcast_to(jnp.sum(update_sum, axis=0, keepdims=True), (M, 128))
    sums = begin([to_cols(i, sc_x.at[k], sc_x.at[k], s_sc.at[i], r_sc.at[i]) for i in range(7)])
    own_col = cols_out.at[y, k]
    cols_x = begin([to_cols(i, own_col, own_col, s_col.at[i], r_col.at[i]) for i in range(7)])
    sent += sums + cols_x

    for n in range(FIRST, len(PARTS)):
        par_copies.append(send_params(n))

    arrive(sums)
    update_sum = sc_x[0]
    for t in range(1, 8):
        update_sum = update_sum + sc_x[t]
    arrive(cols_x)
    own_cols = cols_out.at[pl.ds(y, 1)]
    cols_y = begin(
        [to_line("y", d, own_cols, own_cols, s_col.at[d + 6], r_col.at[d + 6]) for d in LINE_PEERS]
    )
    sent += cols_y
    update_total = update_sum[0:1, 0:1]
    clip = jnp.maximum(1.0, jnp.sqrt(update_total / (M * D * FF)))
    factors = -(RATE * param_scale) / clip * jnp.sqrt(row_mean)
    factor = jnp.zeros((1, 128), F32)
    for m in range(M):
        own_factor = factors[m : m + 1, :]
        factor = factor + jnp.where(lax.rem(iota((1, 128), 1), 8) == m, own_factor, 0.0)
    by_row[...] = factor * jnp.sqrt(rnew[...])
    by_col[0:M, :] = jnp.sqrt(inv_col)

    def block_of_rows(t):
        return pl.ds(pl.multiple_of(t * ROWS, ROWS), ROWS)

    for m in range(M):
        col = by_col[m : m + 1, :]

        def put_change(t, carry, m=m, col=col):
            row = jnp.sum(jnp.where(lane32 == t * 8 + m, by_row[...], 0.0), axis=1, keepdims=True)
            change_out[m, block_of_rows(t), :] = (g_in[t, m].astype(F32) * row) * col
            return carry

        lax.fori_loop(0, 8, put_change, 0)
    arrive(steps)
    own[2 * M].wait()
    arrive(rows_z)
    arrive(cols_y)
    for m in range(M):
        for n, part in enumerate(PARTS):
            if part[0] == m:
                arrive(par_copies[n])
        own[M + m].wait()
        if m == M - 1:
            break

        def put_weights(t, carry, m=m):
            new_out[m, block_of_rows(t), :] = decoded(p_out, s_out, t, m) + change_out[m, block_of_rows(t), :]
            return carry

        lax.fori_loop(0, 8, put_weights, 0)
    for cp in sent:
        cp.wait_send()


def apply_kernel(
    new_ref, change_ref, p_ref, s_ref, rows_ref, cols_ref, map_hbm,
    new_hbm, change_hbm, row_hbm, col_hbm,
    last_buf, row_buf, col_buf, new_map, big_sem, last_sem, small_sem,
):
    fetch = pltpu.make_async_copy(map_hbm, new_map, small_sem.at[0])
    fetch.start()
    big = [pltpu.make_async_copy(change_ref.at[m], change_hbm.at[m], big_sem.at[0, m]) for m in range(M)]
    big += [pltpu.make_async_copy(new_ref.at[m], new_hbm.at[m], big_sem.at[1, m]) for m in range(M - 1)]
    for cp in big:
        cp.start()

    last = []
    for t in range(8):
        rows = pl.ds(t * ROWS, ROWS)
        last_buf[rows, :] = decoded(p_ref, s_ref, t, M - 1) + change_ref[M - 1, rows, :]
        last.append(pltpu.make_async_copy(last_buf.at[rows], new_hbm.at[M - 1, rows], last_sem.at[t]))
        last[-1].start()

    fetch.wait()
    f = lax.axis_index(AXES)
    for n in range(M):
        b = new_map[n, f]
        row_buf[n : n + 1, :] = rows_ref[b // 8, lax.rem(b, 8), n : n + 1, 0:32]
        start = lax.rem(b, 16) * 80
        first = start // 128
        pair = []
        for t in (first, lax.min(first + 1, COLS // 128 - 1)):
            piece = lax.min(t // PIECE, 3)
            at = t - lax.min(piece * PIECE, COLS // 128 - PIECE)
            pair.append(cols_ref[piece, b // 16, n : n + 1, pl.ds(pl.multiple_of(at * 128, 128), 128)])
        pair = jnp.broadcast_to(jnp.concatenate(pair, axis=1), (8, 256))
        take = jnp.where(iota((256, 128), 0) == start - first * 128 + iota((256, 128), 1), 1.0, 0.0)
        got = jnp.dot(pair, take, precision=HIGHEST, preferred_element_type=F32)
        col_buf[n : n + 1, :] = got[0:1, 0:80]
    small = [
        pltpu.make_async_copy(row_buf, row_hbm, small_sem.at[1]),
        pltpu.make_async_copy(col_buf, col_hbm, small_sem.at[2]),
    ]
    for cp in small:
        cp.start()

    for cp in big + last + small:
        cp.wait()


def shards(params, grads, row_state_old, col_state_old, old_map, new_map):
    vmem = pl.BlockSpec(memory_space=pltpu.VMEM)
    hbm = pl.BlockSpec(memory_space=pltpu.HBM)
    dma = pltpu.SemaphoreType.DMA
    given = (params, grads, row_state_old, col_state_old, old_map)
    held = [pltpu.with_memory_space_constraint(a, pltpu.HBM) for a in given]
    held_map = pltpu.with_memory_space_constraint(new_map, pltpu.HBM)
    moved = pl.pallas_call(
        exchange_kernel,
        out_shape=[
            pltpu.VMEM((M - 1, 256, COLS), F32),
            pltpu.VMEM((M, 256, COLS), F32),
            pltpu.VMEM((8, M, ROWS, COLS), jnp.int16),
            pltpu.VMEM((8, M, 256), F32),
            pltpu.VMEM((16, 8, M, 128), F32),
            pltpu.VMEM((4, 8, M, PIECE * 128), F32),
        ],
        in_specs=[hbm] * 5,
        out_specs=[vmem] * 6,
        scratch_shapes=[
            pltpu.VMEM((8, M, ROWS, COLS), jnp.bfloat16),
            pltpu.VMEM((ROWS, 128), F32),
            pltpu.VMEM((8, COLS), F32),
            pltpu.VMEM((M, ROWS, FF), jnp.bfloat16),
            pltpu.VMEM((M, ROWS, FF), F32),
            pltpu.VMEM((8, M, ROWS, COLS), jnp.int16),
            pltpu.VMEM((8, M, 256), F32),
            pltpu.VMEM((M, 32), F32),
            pltpu.VMEM((M, 80), F32),
            pltpu.VMEM((M, 128), jnp.int32),
            pltpu.VMEM((1024, 128), F32),
            pltpu.VMEM((8, M, 128), F32),
            pltpu.VMEM((4, 8, COLS), F32),
            pltpu.VMEM((4, 8, COLS), F32),
            pltpu.VMEM((4, M, 128), F32),
            pltpu.VMEM((4, M, 128), F32),
            pltpu.VMEM((8, M, 128), F32),
            pltpu.VMEM((128, COLS), F32),
            pltpu.VMEM((ROWS, 128), F32),
            dma((2 * M,)),
            dma((3,)),
            dma((2 * M + 1,)),
            dma((7,)), dma((7,)),
            dma((6,)), dma((6,)),
            dma((2, 7)), dma((2, 7)),
            dma((len(PARTS) + 1, 7)), dma((len(PARTS) + 1, 7)),
            dma((7,)), dma((7,)),
            dma((18,)), dma((18,)),
            dma((7,)), dma((7,)),
            dma((10,)), dma((10,)),
        ],
        compiler_params=pltpu.CompilerParams(
            collective_id=0, has_side_effects=True, vmem_limit_bytes=28 << 20
        ),
        name="exchange",
    )(*held)
    return pl.pallas_call(
        apply_kernel,
        out_shape=[
            jax.ShapeDtypeStruct((M, 256, COLS), F32),
            jax.ShapeDtypeStruct((M, 256, COLS), F32),
            jax.ShapeDtypeStruct((M, 32), F32),
            jax.ShapeDtypeStruct((M, 80), F32),
        ],
        in_specs=[vmem] * 6 + [hbm],
        out_specs=[hbm] * 4,
        scratch_shapes=[
            pltpu.VMEM((256, COLS), F32),
            pltpu.VMEM((M, 32), F32),
            pltpu.VMEM((M, 80), F32),
            pltpu.SMEM((M, 128), jnp.int32),
            dma((2, M)),
            dma((8,)),
            dma((3,)),
        ],
        compiler_params=pltpu.CompilerParams(vmem_limit_bytes=28 << 20),
        name="apply",
    )(*(pltpu.with_memory_space_constraint(a, pltpu.VMEM) for a in moved), held_map)


def solution(mesh):
    torus = Mesh(mesh.devices.reshape(4, 4, 4, 2), AXES)
    over = ("z", "y", "x", "c")
    return jax.shard_map(
        shards,
        mesh=torus,
        in_specs=(P(None, over, None), P(None, over, None), P(None, over), P(None, over), P(), P()),
        out_specs=(
            P(None, ("z", "y"), ("x", "c")),
            P(None, ("z", "y"), ("x", "c")),
            P(None, over),
            P(None, over),
        ),
        check_vma=False,
    )
```

time: 76.2 us -> 73.6 us (0.966)
  Pallas kernels: 75.4 us -> 72.8 us
    pallas_call x1, Pallas kernels: 70.6 us -> 68.8 us  [shards(): pl.pallas_call(exchange_kernel, out_shape=[pltpu.VMEM((M - 1, 256, COLS),...]
    pallas_call x1, Pallas kernels: 4.88 us -> 4.09 us  [shards(): pl.pallas_call(apply_kernel, out_shape=[jax.ShapeDtypeStruct((M, 256, COL...]
where the time goes in v5:
time: 73.6 us; the launch traced here: 73.5 us
  Pallas kernels  72.8 us (99%)
    pallas_call x1, Pallas kernels, shards(): pl.pallas_call(exchange_kernel, out_shape=[pltpu.VMEM((M - 1, 256, COLS),...  68.8 us
    pallas_call x1, Pallas kernels, shards(): pl.pallas_call(apply_kernel, out_shape=[jax.ShapeDtypeStruct((M, 256, COL...  4.09 us

profile of v5, /device:TPU:1, one launch (start us, length us, event | category | flops | bytes accessed | tf_op | source)
XLA Modules:
  0.0 73.5 jit_solution(9186730404163881770)
XLA Ops:
  0.6 68.8 %exchange.1 = (f32[3,256,1280]{2,1,0:T(8,128)S(1)}, f32[4,256,1280]{2,1,0:T(8,128)S(1)}, s16[8,4,32,1280]{3,2,1,0:T(8,128)(2,1)S(1)}, f32[8,4,256]{2,1,0:T(4,128...) custom-call(f32[4,32,10240]{2,1,0:T(8,128)} %params.1, bf16[4,32,10240]{2,1,0:T(8,128)(2,1)} %grads.1, ...), custom_call_target="tpu_custom_call" | custom-call | tf_op jit(solution)/shard_map/exchange/pallas_call | solution.py:440
  69.4 4.1 %apply.1 = (f32[4,256,1280]{2,1,0:T(8,128)}, f32[4,256,1280]{2,1,0:T(8,128)}, f32[4,32]{1,0:T(4,128)}, f32[4,80]{1,0:T(4,128)}) custom-call(f32[3,256,1280]{2,1,0:T(8,128)S(1)} %get-tuple-element.10.new_ref, f32[4,256,1280]{2,1,0:T(8,128)S(1)} %get-tuple-element.11.change_ref, s16[8,4,32,1280]{3,2,1,0:T(8,128)(2,1)S(1)} %get-tuple-element.12.p_ref, ...), custom_call_target="tpu_custom_call" | custom-call | tf_op jit(solution)/shard_map/apply/pallas_call | solution.py:489

commit v6 on v5

--- a/solution.py
+++ b/solution.py
@@ -25,6 +25,7 @@
 PIECE = 3
 PARTS = [(0, 0, 32), (1, 0, 32), (2, 0, 16), (2, 16, 16), (3, 0, 32)]
 FIRST = 3
+LEADER = 4
 
 COL_PEERS = [(1, 0), (3, 0), (2, 0), (1, 1), (3, 1), (2, 1), (0, 1)]
 LINE_PEERS = [1, 2, 3]
@@ -43,7 +44,7 @@
     params, grads, row_hbm, col_hbm, map_hbm,
     new_out, change_out, p_out, s_out, rows_out, cols_out,
     g_in, by_row, by_col, gv, pv, qv, sv, row_old, col_old, old_map, stored, row_tiles, red_y, red_z, two_y, two_z, sc_x, sel, rnew,
-    load_sem, small_sem, own_sem,
+    lead_sem, go_sem, load_sem, small_sem, own_sem,
     s_tile, r_tile, s_line, r_line, s_grad, r_grad, s_par, r_par,
     s_row, r_row, s_red, r_red, s_sc, r_sc, s_col, r_col,
 ):
@@ -82,24 +83,37 @@
     for i in range(7):
         tx, tc = col_peer(i)
         pl.semaphore_signal(barrier, inc=1, device_id={"x": tx, "c": tc}, device_id_type=MESH)
-    for d in LINE_PEERS:
-        pl.semaphore_signal(barrier, inc=1, device_id={"y": lax.rem(y + d, 4)}, device_id_type=MESH)
-        pl.semaphore_signal(barrier, inc=1, device_id={"z": lax.rem(z + d, 4)}, device_id_type=MESH)
+
+    def signal_lines(sem):
+        for d in LINE_PEERS:
+            pl.semaphore_signal(sem, inc=1, device_id={"y": lax.rem(y + d, 4)}, device_id_type=MESH)
+            pl.semaphore_signal(sem, inc=1, device_id={"z": lax.rem(z + d, 4)}, device_id_type=MESH)
+
+    @pl.when(k == LEADER)
+    def _():
+        signal_lines(barrier)
+
 
     small = [
         pltpu.make_async_copy(row_hbm, row_old, small_sem.at[0]),
         pltpu.make_async_copy(col_hbm, col_old, small_sem.at[1]),
         pltpu.make_async_copy(map_hbm, old_map, small_sem.at[2]),
     ]
-    begin(small)
     loads = []
     for m in range(M):
         loads.append(pltpu.make_async_copy(grads.at[m], gv.at[m], load_sem.at[m]))
     for m in range(M):
         loads.append(pltpu.make_async_copy(params.at[m], pv.at[m], load_sem.at[M + m]))
-    begin(loads)
-
-    pl.semaphore_wait(barrier, 13)
+    begin(loads[0:1] + small + loads[1:])
+
+    @pl.when(k == LEADER)
+    def _():
+        pl.semaphore_wait(barrier, 13)
+
+    @pl.when(k != LEADER)
+    def _():
+        pl.semaphore_wait(barrier, 7)
+
 
     def columns(i):
         tx, tc = col_peer(i)
@@ -107,13 +121,19 @@
 
     def send_grads(first, count, n):
         part = pl.ds(first, count)
+        for m in range(first, first + count):
+            loads[m].wait()
         copies = [
-            to_cols(i, grads.at[part, :, columns(i)], g_in.at[k, part], s_grad.at[n, i], r_grad.at[n, i])
+            to_cols(i, gv.at[part, :, columns(i)], g_in.at[k, part], s_grad.at[n, i], r_grad.at[n, i])
             for i in range(7)
         ]
         return begin(copies)
 
     grad_copies = send_grads(0, 1, 0)
+
+    @pl.when(k == LEADER)
+    def _():
+        signal_lines(lead_sem)
 
     mine = stored.at[pl.ds(pl.multiple_of(f * 8, 8), 8)]
     mine[...] = jnp.zeros((8, 128), F32)
@@ -148,7 +168,6 @@
     row_sums = jnp.zeros((ROWS, 128), F32)
     own = []
     for m in range(M):
-        loads[m].wait()
 
         def add_squares(t, acc, m=m):
             g = gv[m, :, pl.ds(pl.multiple_of(t * COLS, 128), COLS)].astype(F32)
@@ -196,6 +215,18 @@
     sent += steps
 
     arrive(tiles)
+
+    @pl.when(k == LEADER)
+    def _():
+        pl.semaphore_wait(lead_sem, 6)
+        for i in range(7):
+            tx, tc = col_peer(i)
+            pl.semaphore_signal(go_sem, inc=1, device_id={"x": tx, "c": tc}, device_id_type=MESH)
+
+    @pl.when(k != LEADER)
+    def _():
+        pl.semaphore_wait(go_sem, 1)
+
     line_at = stored.at[pl.ds(pl.multiple_of((z * 4 + y) * 64, 64), 64)]
     lines = begin([to_line("y", d, line_at, line_at, s_line.at[d - 1], r_line.at[d - 1]) for d in LINE_PEERS])
     sent += lines
@@ -469,6 +500,8 @@
             pltpu.VMEM((8, M, 128), F32),
             pltpu.VMEM((128, COLS), F32),
             pltpu.VMEM((ROWS, 128), F32),
+            pltpu.SemaphoreType.REGULAR,
+            pltpu.SemaphoreType.REGULAR,
             dma((2 * M,)),
             dma((3,)),
             dma((2 * M + 1,)),

time: 73.6 us -> 71.5 us (0.971)
  Pallas kernels: 72.8 us -> 70.7 us
    pallas_call x1, Pallas kernels: 68.8 us -> 66.6 us  [shards(): pl.pallas_call(exchange_kernel, out_shape=[pltpu.VMEM((M - 1, 256, COLS),...]
where the time goes in v6:
time: 71.5 us; the launch traced here: 71.3 us
  Pallas kernels  70.7 us (99%)
    pallas_call x1, Pallas kernels, shards(): pl.pallas_call(exchange_kernel, out_shape=[pltpu.VMEM((M - 1, 256, COLS),...  66.6 us
    pallas_call x1, Pallas kernels, shards(): pl.pallas_call(apply_kernel, out_shape=[jax.ShapeDtypeStruct((M, 256, COL...  4.09 us

profile of v6, /device:TPU:1, one launch (start us, length us, event | category | flops | bytes accessed | tf_op | source)
XLA Modules:
  0.0 71.3 jit_solution(14407368536899130755)
XLA Ops:
  0.6 66.6 %exchange.1 = (f32[3,256,1280]{2,1,0:T(8,128)S(1)}, f32[4,256,1280]{2,1,0:T(8,128)S(1)}, s16[8,4,32,1280]{3,2,1,0:T(8,128)(2,1)S(1)}, f32[8,4,256]{2,1,0:T(4,128...) custom-call(f32[4,32,10240]{2,1,0:T(8,128)} %params.1, bf16[4,32,10240]{2,1,0:T(8,128)(2,1)} %grads.1, ...), custom_call_target="tpu_custom_call" | custom-call | tf_op jit(solution)/shard_map/exchange/pallas_call | solution.py:471
  67.2 4.1 %apply.1 = (f32[4,256,1280]{2,1,0:T(8,128)}, f32[4,256,1280]{2,1,0:T(8,128)}, f32[4,32]{1,0:T(4,128)}, f32[4,80]{1,0:T(4,128)}) custom-call(f32[3,256,1280]{2,1,0:T(8,128)S(1)} %get-tuple-element.10.new_ref, f32[4,256,1280]{2,1,0:T(8,128)S(1)} %get-tuple-element.11.change_ref, s16[8,4,32,1280]{3,2,1,0:T(8,128)(2,1)S(1)} %get-tuple-element.12.p_ref, ...), custom_call_target="tpu_custom_call" | custom-call | tf_op jit(solution)/shard_map/apply/pallas_call | solution.py:522

commit v7 on v6

--- a/solution.py
+++ b/solution.py
@@ -27,7 +27,9 @@
 FIRST = 3
 LEADER = 4
 
-COL_PEERS = [(1, 0), (3, 0), (2, 0), (1, 1), (3, 1), (2, 1), (0, 1)]
+COL_PEERS = [(1, 0), (3, 0), (1, 1), (3, 1), (0, 1), (2, 0), (2, 1)]
+NEAR = 5
+ORDER = (0, 1, 5, 2, 3, 6, 4)
 LINE_PEERS = [1, 2, 3]
 
 
@@ -36,17 +38,17 @@
 
 
 def decoded(codes, steps, t, m):
-    step = jnp.concatenate([steps[t, m : m + 1, :]] * (COLS // 256), axis=1)
+    step = jnp.concatenate([steps[t, m : m + 1, 0:256]] * (COLS // 256), axis=1)
     return codes[t, m].astype(jnp.int32).astype(F32) * step
 
 
 def exchange_kernel(
     params, grads, row_hbm, col_hbm, map_hbm,
     new_out, change_out, p_out, s_out, rows_out, cols_out,
-    g_in, by_row, by_col, gv, pv, qv, sv, row_old, col_old, old_map, stored, row_tiles, red_y, red_z, two_y, two_z, sc_x, sel, rnew,
-    lead_sem, go_sem, load_sem, small_sem, own_sem,
+    g_in, by_row, by_col, gv, pv, qv, sv, row_old, col_old, old_map, stored, red_y, red_z, two_y, two_z, sel, rnew,
+    far_sem, lead_sem, go_sem, load_sem, small_sem, own_sem,
     s_tile, r_tile, s_line, r_line, s_grad, r_grad, s_par, r_par,
-    s_row, r_row, s_red, r_red, s_sc, r_sc, s_col, r_col,
+    s_row, r_row, s_red, r_red, s_col, r_col,
 ):
     z, y, x, c = (lax.axis_index(a) for a in AXES)
     k = x * 2 + c
@@ -80,7 +82,7 @@
             cp.wait_recv()
 
     barrier = pltpu.get_barrier_semaphore()
-    for i in range(7):
+    for i in range(NEAR):
         tx, tc = col_peer(i)
         pl.semaphore_signal(barrier, inc=1, device_id={"x": tx, "c": tc}, device_id_type=MESH)
 
@@ -108,28 +110,30 @@
 
     @pl.when(k == LEADER)
     def _():
-        pl.semaphore_wait(barrier, 13)
+        pl.semaphore_wait(barrier, NEAR + 6)
 
     @pl.when(k != LEADER)
     def _():
-        pl.semaphore_wait(barrier, 7)
+        pl.semaphore_wait(barrier, NEAR)
 
 
     def columns(i):
         tx, tc = col_peer(i)
         return pl.ds(pl.multiple_of((tx * 2 + tc) * COLS, 128), COLS)
 
-    def send_grads(first, count, n):
+    def send_grads(first, count, n, peers):
         part = pl.ds(first, count)
-        for m in range(first, first + count):
-            loads[m].wait()
         copies = [
             to_cols(i, gv.at[part, :, columns(i)], g_in.at[k, part], s_grad.at[n, i], r_grad.at[n, i])
-            for i in range(7)
+            for i in peers
         ]
         return begin(copies)
 
-    grad_copies = send_grads(0, 1, 0)
+    pl.semaphore_signal(far_sem, inc=1, device_id={"x": lax.rem(x + 3, 4)}, device_id_type=MESH)
+    loads[0].wait()
+    grad_copies = send_grads(0, 1, 0, range(NEAR))
+    pl.semaphore_wait(far_sem, 1)
+    grad_copies += send_grads(0, 1, 0, range(NEAR, 7))
 
     @pl.when(k == LEADER)
     def _():
@@ -143,7 +147,9 @@
     mine[4:8, 0:32] = row_old[...]
 
     tiles = begin([to_cols(i, mine, mine, s_tile.at[i], r_tile.at[i]) for i in range(7)])
-    grad_copies += send_grads(1, M - 1, 1)
+    for m in range(1, M):
+        loads[m].wait()
+    grad_copies += send_grads(1, M - 1, 1, ORDER)
     sent = tiles + grad_copies
 
     def peer_block(i):
@@ -156,7 +162,7 @@
         copies = begin(
             [
                 to_cols(i, qv.at[peer_block(i), m, rows], p_out.at[k, m, rows], s_par.at[n, i], r_par.at[n, i])
-                for i in range(7)
+                for i in ORDER
             ]
         )
         sent.extend(copies)
@@ -199,7 +205,7 @@
                     tops[u % 2] = jnp.maximum(tops[u % 2], size[v * 8 : (v + 1) * 8, u * 128 : (u + 1) * 128])
             top = jnp.concatenate([jnp.max(a, axis=0, keepdims=True) for a in tops], axis=1)
             top = jnp.maximum(top, 1e-30)
-            sv[t, m : m + 1, :] = top * (1.0 / TOP)
+            sv[t, m : m + 1, 0:256] = top * (1.0 / TOP)
             per = jnp.concatenate([TOP / top] * (COLS // 256), axis=1)
             qv[t, m] = jnp.round(w * per).astype(jnp.int32).astype(jnp.int16)
             return acc
@@ -209,10 +215,6 @@
         squares = squares + jnp.where((at8 == m) & (lane8 == ROWS), total, 0.0)
         own.append(pltpu.make_async_copy(qv.at[k, m], p_out.at[k, m], own_sem.at[M + m]))
         own[-1].start()
-    own.append(pltpu.make_async_copy(sv.at[k], s_out.at[k], own_sem.at[2 * M]))
-    own[-1].start()
-    steps = begin([to_cols(i, sv.at[peer_block(i)], s_out.at[k], s_par.at[len(PARTS), i], r_par.at[len(PARTS), i]) for i in range(7)])
-    sent += steps
 
     arrive(tiles)
 
@@ -249,9 +251,11 @@
     row_sums = jnp.transpose(sel[:, 0:128])[0:8, :]
     row_new = DECAY * picked[0:8, :] + (1.0 - DECAY) * row_sums / FF
     row_new = jnp.where((at8 < M) & (lane8 < ROWS), row_new, 1.0)
-    own_tile = row_tiles.at[k]
-    own_tile[...] = jnp.where(lane8 == ROWS, squares, row_new)[0:M, :]
-    row_copies = begin([to_cols(i, own_tile, own_tile, s_row.at[i], r_row.at[i]) for i in range(7)])
+    own_tile = jnp.where(lane8 == ROWS, squares, row_new)[0:M, :]
+    for t in range(8):
+        sv[t, :, 256:384] = own_tile
+    s_out[k] = sv[k]
+    row_copies = begin([to_cols(i, sv.at[peer_block(i)], s_out.at[k], s_row.at[i], r_row.at[i]) for i in range(7)])
     sent += row_copies
     for n in range(FIRST):
         par_copies.append(send_params(n))
@@ -284,18 +288,19 @@
     for m in range(M):
         own[m].wait()
     arrive(row_copies)
-    tile_sum = row_tiles[0]
+    tile_sum = s_out[0, :, 256:384]
     for t in range(1, 8):
-        tile_sum = tile_sum + row_tiles[t]
+        tile_sum = tile_sum + s_out[t, :, 256:384]
     lane4 = iota((M, 128), 1)
     row_sum = jnp.sum(jnp.where(lane4 < ROWS, tile_sum, 0.0), axis=1, keepdims=True)
     weight_sum = jnp.sum(jnp.where(lane4 == ROWS, tile_sum, 0.0), axis=1, keepdims=True)
     two_y[y] = jnp.where(lane4 == 0, row_sum, jnp.where(lane4 == 1, weight_sum, 0.0))
     own_row = z * 4 + y
-    rows_out[own_row] = row_tiles[...]
+    for t in range(8):
+        rows_out[own_row, t] = s_out[t, :, 256:384]
     sel[:, 128:256] = jnp.ones((128, 128), F32)
     for t in range(8):
-        sel[t * 8 : t * 8 + M, 128:256] = row_tiles[t]
+        sel[t * 8 : t * 8 + M, 128:256] = s_out[t, :, 256:384]
     rnew[...] = 1.0 / jnp.transpose(sel[:, 128:256])[0:ROWS, :]
 
     for m in range(M):
@@ -349,24 +354,22 @@
     col_new = DECAY * by_col[0:M, :] + (1.0 - DECAY) * total[0:M, :] / D
     sel[0:M, :] = col_new
     piece = lax.min(y * PIECE, COLS // 128 - PIECE)
-    cols_out[y, k] = sel[0:M, pl.ds(pl.multiple_of(piece * 128, 128), PIECE * 128)]
+    cols_out[y, k, :, 0 : PIECE * 128] = sel[0:M, pl.ds(pl.multiple_of(piece * 128, 128), PIECE * 128)]
     inv_col = 1.0 / col_new
 
     update_sum = jnp.sum(total[M : 2 * M, :] * inv_col, axis=1, keepdims=True) * row_mean
-    sc_x[k] = jnp.broadcast_to(jnp.sum(update_sum, axis=0, keepdims=True), (M, 128))
-    sums = begin([to_cols(i, sc_x.at[k], sc_x.at[k], s_sc.at[i], r_sc.at[i]) for i in range(7)])
+    cols_out[y, k, :, PIECE * 128 :] = jnp.broadcast_to(jnp.sum(update_sum, axis=0, keepdims=True), (M, 128))
     own_col = cols_out.at[y, k]
     cols_x = begin([to_cols(i, own_col, own_col, s_col.at[i], r_col.at[i]) for i in range(7)])
-    sent += sums + cols_x
+    sent += cols_x
 
     for n in range(FIRST, len(PARTS)):
         par_copies.append(send_params(n))
 
-    arrive(sums)
-    update_sum = sc_x[0]
+    arrive(cols_x)
+    update_sum = cols_out[y, 0, 0:1, PIECE * 128 :]
     for t in range(1, 8):
-        update_sum = update_sum + sc_x[t]
-    arrive(cols_x)
+        update_sum = update_sum + cols_out[y, t, 0:1, PIECE * 128 :]
     own_cols = cols_out.at[pl.ds(y, 1)]
     cols_y = begin(
         [to_line("y", d, own_cols, own_cols, s_col.at[d + 6], r_col.at[d + 6]) for d in LINE_PEERS]
@@ -394,8 +397,6 @@
             return carry
 
         lax.fori_loop(0, 8, put_change, 0)
-    arrive(steps)
-    own[2 * M].wait()
     arrive(rows_z)
     arrive(cols_y)
     for m in range(M):
@@ -474,9 +475,9 @@
             pltpu.VMEM((M - 1, 256, COLS), F32),
             pltpu.VMEM((M, 256, COLS), F32),
             pltpu.VMEM((8, M, ROWS, COLS), jnp.int16),
-            pltpu.VMEM((8, M, 256), F32),
+            pltpu.VMEM((8, M, 384), F32),
             pltpu.VMEM((16, 8, M, 128), F32),
-            pltpu.VMEM((4, 8, M, PIECE * 128), F32),
+            pltpu.VMEM((4, 8, M, (PIECE + 1) * 128), F32),
         ],
         in_specs=[hbm] * 5,
         out_specs=[vmem] * 6,
@@ -487,31 +488,29 @@
             pltpu.VMEM((M, ROWS, FF), jnp.bfloat16),
             pltpu.VMEM((M, ROWS, FF), F32),
             pltpu.VMEM((8, M, ROWS, COLS), jnp.int16),
-            pltpu.VMEM((8, M, 256), F32),
+            pltpu.VMEM((8, M, 384), F32),
             pltpu.VMEM((M, 32), F32),
             pltpu.VMEM((M, 80), F32),
             pltpu.VMEM((M, 128), jnp.int32),
             pltpu.VMEM((1024, 128), F32),
-            pltpu.VMEM((8, M, 128), F32),
             pltpu.VMEM((4, 8, COLS), F32),
             pltpu.VMEM((4, 8, COLS), F32),
             pltpu.VMEM((4, M, 128), F32),
             pltpu.VMEM((4, M, 128), F32),
-            pltpu.VMEM((8, M, 128), F32),
             pltpu.VMEM((128, COLS), F32),
             pltpu.VMEM((ROWS, 128), F32),
             pltpu.SemaphoreType.REGULAR,
             pltpu.SemaphoreType.REGULAR,
+            pltpu.SemaphoreType.REGULAR,
             dma((2 * M,)),
             dma((3,)),
-            dma((2 * M + 1,)),
+            dma((2 * M,)),
             dma((7,)), dma((7,)),
             dma((6,)), dma((6,)),
             dma((2, 7)), dma((2, 7)),
-            dma((len(PARTS) + 1, 7)), dma((len(PARTS) + 1, 7)),
+            dma((len(PARTS), 7)), dma((len(PARTS), 7)),
             dma((7,)), dma((7,)),
             dma((18,)), dma((18,)),
-            dma((7,)), dma((7,)),
             dma((10,)), dma((10,)),
         ],
         compiler_params=pltpu.CompilerParams(

time: 71.5 us -> 71 us (level)
  no operation moved by 1% of the time
where the time goes in v7:
time: 71 us; the launch traced here: 70.9 us
  Pallas kernels  70.2 us (99%)
    pallas_call x1, Pallas kernels, shards(): pl.pallas_call(exchange_kernel, out_shape=[pltpu.VMEM((M - 1, 256, COLS),...  66.2 us
    pallas_call x1, Pallas kernels, shards(): pl.pallas_call(apply_kernel, out_shape=[jax.ShapeDtypeStruct((M, 256, COL...  4.09 us

profile of v7, /device:TPU:1, one launch (start us, length us, event | category | flops | bytes accessed | tf_op | source)
XLA Modules:
  0.0 70.9 jit_solution(10520102839932372788)
XLA Ops:
  0.6 66.2 %exchange.1 = (f32[3,256,1280]{2,1,0:T(8,128)S(1)}, f32[4,256,1280]{2,1,0:T(8,128)S(1)}, s16[8,4,32,1280]{3,2,1,0:T(8,128)(2,1)S(1)}, f32[8,4,384]{2,1,0:T(4,128...) custom-call(f32[4,32,10240]{2,1,0:T(8,128)} %params.1, bf16[4,32,10240]{2,1,0:T(8,128)(2,1)} %grads.1, ...), custom_call_target="tpu_custom_call" | custom-call | tf_op jit(solution)/shard_map/exchange/pallas_call | solution.py:472
  66.8 4.1 %apply.1 = (f32[4,256,1280]{2,1,0:T(8,128)}, f32[4,256,1280]{2,1,0:T(8,128)}, f32[4,32]{1,0:T(4,128)}, f32[4,80]{1,0:T(4,128)}) custom-call(f32[3,256,1280]{2,1,0:T(8,128)S(1)} %get-tuple-element.10.new_ref, f32[4,256,1280]{2,1,0:T(8,128)S(1)} %get-tuple-element.11.change_ref, s16[8,4,32,1280]{3,2,1,0:T(8,128)(2,1)S(1)} %get-tuple-element.12.p_ref, ...), custom_call_target="tpu_custom_call" | custom-call | tf_op jit(solution)/shard_map/apply/pallas_call | solution.py:521

commit v8 on v7

--- a/solution.py
+++ b/solution.py
@@ -23,7 +23,7 @@
 F32 = jnp.float32
 TOP = 32767.0
 PIECE = 3
-PARTS = [(0, 0, 32), (1, 0, 32), (2, 0, 16), (2, 16, 16), (3, 0, 32)]
+PARTS = [(0, 0, 32), (1, 0, 32), (2, 0, 16), (2, 16, 16), (3, 0, 16), (3, 16, 16)]
 FIRST = 3
 LEADER = 4
 

time: 71 us -> 71.2 us (level)
  no operation moved by 1% of the time
where the time goes in v8:
time: 71.2 us; the launch traced here: 71 us
  Pallas kernels  70.4 us (99%)
    pallas_call x1, Pallas kernels, shards(): pl.pallas_call(exchange_kernel, out_shape=[pltpu.VMEM((M - 1, 256, COLS),...  66.3 us
    pallas_call x1, Pallas kernels, shards(): pl.pallas_call(apply_kernel, out_shape=[jax.ShapeDtypeStruct((M, 256, COL...  4.09 us

profile of v8, /device:TPU:1, one launch (start us, length us, event | category | flops | bytes accessed | tf_op | source)
XLA Modules:
  0.0 71.0 jit_solution(7088853076442544452)
XLA Ops:
  0.6 66.3 %exchange.1 = (f32[3,256,1280]{2,1,0:T(8,128)S(1)}, f32[4,256,1280]{2,1,0:T(8,128)S(1)}, s16[8,4,32,1280]{3,2,1,0:T(8,128)(2,1)S(1)}, f32[8,4,384]{2,1,0:T(4,128...) custom-call(f32[4,32,10240]{2,1,0:T(8,128)} %params.1, bf16[4,32,10240]{2,1,0:T(8,128)(2,1)} %grads.1, ...), custom_call_target="tpu_custom_call" | custom-call | tf_op jit(solution)/shard_map/exchange/pallas_call | solution.py:472
  66.9 4.1 %apply.1 = (f32[4,256,1280]{2,1,0:T(8,128)}, f32[4,256,1280]{2,1,0:T(8,128)}, f32[4,32]{1,0:T(4,128)}, f32[4,80]{1,0:T(4,128)}) custom-call(f32[3,256,1280]{2,1,0:T(8,128)S(1)} %get-tuple-element.10.new_ref, f32[4,256,1280]{2,1,0:T(8,128)S(1)} %get-tuple-element.11.change_ref, s16[8,4,32,1280]{3,2,1,0:T(8,128)(2,1)S(1)} %get-tuple-element.12.p_ref, ...), custom_call_target="tpu_custom_call" | custom-call | tf_op jit(solution)/shard_map/apply/pallas_call | solution.py:521
